TPU v7x, 32 devices: a whole 2x2x4 slice. The times are simulated.
32 devices in a mesh: users: 16 (over z, y, x), cols: 2 (over core).
Axes of the slice: x: 2, y: 2, z: 4, core: 2. Of those that a mesh axis runs over, the one named last changes fastest.
Arguments:
- item_ids: int32 [256, 256], P('users'), may hold values from 0 to 32767, as said below
- lengths: int32 [256], P('users'), may hold values from 1 to 256, 40960 in all
- seed_rows: int32 [256, 256], P('users'), may hold values from 0 to 63
- item_table: bfloat16 [32768, 1024], P('users', 'cols'), may hold values from -0.59765625 to 0.59765625
- bilinear: bfloat16 [1024, 1024], P(None, 'cols'), may hold values from -0.1875 to 0.1875
- seed_table: float32 [64, 8], replicated, may hold values from -260 to 260
Outputs:
- capsules: float32 [256, 8, 1024], P('users', None, 'cols')
Inputs may be any that keep to these rules, and one draw needn't show every extreme that they name: `item_ids`: ids 2048 * s to 2048 * (s + 1) - 1 form table shard s. Of the 4096 ids of one index of users, at most 512 lie in one shard, and exactly 512 lie in some shard.
All inputs are finite; a program needn't handle non-finite values. No bound on the sum of `lengths` on one device may be relied on, other than what follows from the above.
Results may differ from a plain program's by a relative error of at most 0.0046.
Values may be sent and summed in bfloat16 or wider, within the bound.
No kernel may reach another device: no remote copies, remote signals or barrier semaphores. Data moves between devices by JAX's collectives and lax.ppermute only.
A program may use at most 128 MiB of HBM per device.

v0:
```python
import jax
import jax.numpy as jnp
from jax import lax
from jax.sharding import PartitionSpec as P

ITERS = 3


def squash_scale(squares):
    return squares / (1.0 + squares) / jnp.sqrt(squares + 1e-06)


def owner_ranks(owner, owners):
    tok_count = owner.shape[0]
    span = min(256, tok_count)
    onehot = (owner[:, None] == jnp.arange(owners, dtype=jnp.int32)[None, :]).astype(jnp.float32)
    blocked = onehot.reshape(tok_count // span, span, owners)
    row_ids = lax.broadcasted_iota(jnp.int32, (span, span), 0)
    col_ids = lax.broadcasted_iota(jnp.int32, (span, span), 1)
    lower = (row_ids >= col_ids).astype(jnp.float32)
    within = jnp.einsum("ij,bjo->bio", lower, blocked)
    totals = within[:, -1, :]
    before = jnp.cumsum(totals, axis=0) - totals
    counts = (within + before[:, None, :]).reshape(tok_count, owners)
    return (jnp.sum(counts * onehot, axis=1) - 1.0).astype(jnp.int32)


def on_device(item_ids, lengths, seed_rows, item_table, bilinear, seed_table):
    users_here, hist = item_ids.shape
    owners = lax.axis_size("users")
    rows_dev = item_table.shape[0]
    half = bilinear.shape[1]
    tok_count = users_here * hist
    capacity = max(2, (2 * tok_count + owners - 1) // owners)
    flat_ids = item_ids.reshape(tok_count)
    owner = flat_ids // rows_dev
    row_in = flat_ids % rows_dev
    slot = owner * capacity + owner_ranks(owner, owners)
    requests = (
        jnp.zeros((owners * capacity,), jnp.int32).at[slot].set(row_in).reshape(owners, capacity)
    )
    answers = lax.all_to_all(
        item_table[lax.all_to_all(requests, "users", split_axis=0, concat_axis=0, tiled=True)],
        "users",
        split_axis=0,
        concat_axis=0,
        tiled=True,
    )
    halves = answers.reshape(owners * capacity, half)[slot]
    embedded = lax.all_gather(halves, "cols", axis=1, tiled=True)
    mapped = jnp.dot(embedded, bilinear, preferred_element_type=jnp.float32).astype(jnp.bfloat16)
    mapped = mapped.reshape(users_here, hist, half)
    seeds = seed_table.shape[0]
    seed_onehot = (
        seed_rows.reshape(tok_count)[:, None] == jnp.arange(seeds, dtype=jnp.int32)[None, :]
    ).astype(jnp.float32)
    logits = jnp.dot(seed_onehot, seed_table, precision=lax.Precision.HIGHEST).reshape(
        users_here, hist, -1
    )
    position = jnp.arange(hist, dtype=jnp.int32)
    live = (position[None, :] < lengths[:, None]).astype(jnp.float32)
    capsules = jnp.zeros((users_here, logits.shape[2], half), jnp.float32)
    for step in range(ITERS):
        weights = (jax.nn.softmax(logits, axis=-1) * live[:, :, None]).astype(jnp.bfloat16)
        summed = jnp.einsum("utk,utd->ukd", weights, mapped, preferred_element_type=jnp.float32)
        partial_value = jnp.sum(summed * summed, axis=-1)
        if step + 1 < ITERS:
            products = jnp.einsum(
                "utd,ukd->utk",
                mapped,
                summed,
                preferred_element_type=jnp.float32,
                precision=lax.Precision.HIGHEST,
            )
            squares, dots = lax.psum((partial_value, products), "cols")
            scale = squash_scale(squares)
            logits = logits + dots * scale[:, None, :]
        else:
            squares = lax.psum(partial_value, "cols")
            scale = squash_scale(squares)
        capsules = summed * scale[:, :, None]
    return capsules


def solution(mesh):
    placed = (
        P("users", None),
        P("users"),
        P("users", None),
        P("users", "cols"),
        P(None, "cols"),
        P(),
    )
    return jax.shard_map(
        on_device, mesh=mesh, in_specs=placed, out_specs=P("users", None, "cols"), check_vma=False
    )
```

profile of v0, /device:TPU:0, one launch (start us, length us, event | category | flops | bytes accessed | tf_op | source)
XLA Modules:
  0.0 385.6 jit_solution(16573011084870048128)
XLA Ops:
  6.5 0.9 add_select_fusion.1
  7.4 0.2 convolution_bitcast_fusion
  7.7 0.1 copy.9
  7.9 0.2 copy.10
  8.1 0.2 subtract_reduce_fusion
  8.3 0.1 select_reduce_fusion
  8.5 0.7 copy.12
  9.2 0.7 copy.14
  10.1 15.5 %scatter_custom_fusion = s32[8192]{0:T(1024)S(1)} fusion(s32[4096]{0:T(1024)S(1)} %bitcast.52, s32[4096]{0:T(1024)S(1)} %add_select_fusion, s32[]{:T(128)} %constant.39.clone.1), kind=kCustom, calls=%fused_computation.60 | custom fusion | bytes 32772 | tf_op jit(solution)/shard_map/scatter | solution.py:40
  25.6 15.5 %all_to_all.17 = s32[16,1,512]{2,1,0:T(1,128)S(1)} all-to-all(s32[16,1,512]{2,1,0:T(1,128)S(1)} %bitcast.50), channel_id=1, replica_groups=mesh['users'=16,'cols'=2] {'users'}, dimensions={0} | all-to-all | bytes 65536 | tf_op jit(solution)/shard_map/all_to_all | solution.py:43
  41.3 33.6 %gather_fusion = bf16[8192,512]{1,0:T(8,128)(2,1)} fusion(bf16[2048,512]{1,0:T(8,128)(2,1)S(1)} %copy-done, s32[8192]{0:T(1024)S(1)} %broadcast_clamp_fusion), kind=kCustom, calls=%fused_computation | custom fusion | bytes 16809984 | tf_op jit(solution)/shard_map/gather | solution.py:43
  74.8 4.7 %all-to-all-start.1 = ((bf16[16,512,512]{2,1,0:T(8,128)(2,1)}), bf16[16,512,512]{2,1,0:T(8,128)(2,1)}, u32[]{:S(2)}, u32[]{:S(2)}) async-start(bf16[16,512,512]{2,1,0:T(8,128)(2,1)} %bitcast.45), calls=%async_computation.1 | async-start | bytes 16777216 | tf_op jit(solution)/shard_map/all_to_all | solution.py:42
  79.6 153.7 %all-to-all-done.1 = bf16[16,512,512]{2,1,0:T(8,128)(2,1)} async-done(((bf16[16,512,512]{2,1,0:T(8,128)(2,1)}), bf16[16,512,512]{2,1,0:T(8,128)(2,1)}, u32[]{:S(2)}, u32[]{:S(2)}) %all-to-all-start.1) | async-done | bytes 8388640 | tf_op jit(solution)/shard_map/all_to_all | solution.py:42
  233.4 21.9 %gather_fusion.1 = bf16[4096,512]{1,0:T(8,128)(2,1)} fusion(bf16[8192,512]{1,0:T(8,128)(2,1)} %bitcast.8, s32[4096]{0:T(1024)S(1)} %broadcast_clamp_fusion.1), kind=kCustom, calls=%fused_computation.1 | custom fusion | bytes 8404992 | tf_op jit(solution)/shard_map/gather | solution.py:49
  255.3 0.6 copy-done.2
  256.0 1.9 fusion.31
  258.1 50.9 %all-gather.3.cloned.1.call-done = bf16[4096,1024]{1,0:T(8,128)(2,1)} async-done(((bf16[4096,512]{1,0:T(8,128)(2,1)}), bf16[4096,1024]{1,0:T(8,128)(2,1)}) %all-gather.3.cloned.1.call-update) | async-done | bytes 8388624 | tf_op jit(solution)/shard_map/all_gather | solution.py:50
  309.0 8.1 %convolution_convert_fusion = bf16[4096,512]{1,0:T(8,128)(2,1)S(1)} fusion(bf16[4096,1024]{1,0:T(8,128)(2,1)} %all-gather.3.cloned.1.call-done, bf16[1024,512]{1,0:T(8,128)(2,1)S(1)} %copy-done.4), kind=kOutput, calls=%fused_computation.5 | convolution fusion | flops 4297064448 | bytes 13631488 | tf_op jit(solution)/shard_map/dot_general | solution.py:51
  317.1 0.7 multiply_reduce_fusion.2
  317.9 1.2 copy-done.1
  319.0 4.0 %fusion.35 = f32[16,256,8]{1,2,0:T(8,128)} fusion(bf16[16,256,512]{2,1,0:T(8,128)(2,1)S(1)} %bitcast.41, f32[16,8,512]{2,1,0:T(8,128)S(1)} %get-tuple-element.8), kind=kOutput, calls=%fused_computation.75 | convolution fusion | flops 201326592 | bytes 4587520 | tf_op jit(solution)/shard_map/utd,ukd->utk/dot_general | solution.py:68
  323.1 2.5 psum.36
  325.6 16.7 %all-reduce.3.cloned.1.call-done = f32[16,256,8]{1,2,0:T(8,128)} async-done(((f32[16,256,8]{1,2,0:T(8,128)}), f32[16,256,8]{1,2,0:T(8,128)}) %all-reduce.3.cloned.1.call-update) | async-done | bytes 131088 | tf_op jit(solution)/shard_map/psum | solution.py:75
  342.3 1.0 multiply_add_fusion.1
  343.4 2.9 multiply_reduce_fusion.1
  346.3 6.2 %fusion.36 = f32[16,256,8]{1,2,0:T(8,128)} fusion(bf16[16,256,512]{2,1,0:T(8,128)(2,1)} %bitcast.43, f32[16,8,512]{2,1,0:T(8,128)S(1)} %get-tuple-element.10), kind=kOutput, calls=%fused_computation.76 | convolution fusion | flops 201326592 | bytes 4587520 | tf_op jit(solution)/shard_map/utd,ukd->utk/dot_general | solution.py:68
  352.5 2.5 psum.38
  355.1 16.8 %all-reduce.5.cloned.1.call-done = f32[16,256,8]{1,2,0:T(8,128)} async-done(((f32[16,256,8]{1,2,0:T(8,128)}), f32[16,256,8]{1,2,0:T(8,128)}) %all-reduce.5.cloned.1.call-update) | async-done | bytes 131088 | tf_op jit(solution)/shard_map/psum | solution.py:75
  371.8 1.1 fusion.33
  372.9 2.9 multiply_reduce_fusion
  375.8 2.5 psum.39
  378.3 0.8 broadcast_multiply_fusion
  (34 shorter events, 0.8 us)
Async XLA Ops:
  6.5 34.7 %copy-start = (bf16[2048,512]{1,0:T(8,128)(2,1)S(1)}, bf16[2048,512]{1,0:T(8,128)(2,1)}, u32[]{:S(2)}) copy-start(bf16[2048,512]{1,0:T(8,128)(2,1)} %param.9) | copy-start | bytes 6291460
  74.8 158.6 %all-to-all-start.1 = ((bf16[16,512,512]{2,1,0:T(8,128)(2,1)}), bf16[16,512,512]{2,1,0:T(8,128)(2,1)}, u32[]{:S(2)}, u32[]{:S(2)}) async-start(bf16[16,512,512]{2,1,0:T(8,128)(2,1)} %bitcast.45), calls=%async_computation.1 | async-start | bytes 16777216 | tf_op jit(solution)/shard_map/all_to_all | solution.py:42
  79.6 229.4 %all-gather.3.cloned.1.call-start = ((), (), s32[]{:S(2)}) async-start(), calls=%async_computation.4 | async-start | bytes 12582912 | tf_op jit(solution)/shard_map/all_gather | solution.py:50
  255.2 0.7 copy-start.2
  255.2 0.7 copy-start.5
  255.2 2.8 copy-start.3
  255.3 53.8 %copy-start.4 = (bf16[1024,512]{1,0:T(8,128)(2,1)S(1)}, bf16[1024,512]{1,0:T(8,128)(2,1)}, u32[]{:S(2)}) copy-start(bf16[1024,512]{1,0:T(8,128)(2,1)} %param.10) | copy-start | bytes 3145732
  255.3 87.0 %all-reduce.3.cloned.1.call-start = ((), (), s32[]{:S(2)}) async-start(), calls=%async_computation.2 | async-start | bytes 262144 | tf_op jit(solution)/shard_map/psum | solution.py:75
  317.1 1.9 copy-start.1
  323.1 48.8 %all-reduce.5.cloned.1.call-start = ((), (), s32[]{:S(2)}) async-start(), calls=%async_computation.3 | async-start | bytes 262144 | tf_op jit(solution)/shard_map/psum | solution.py:75
Sparse Core Ops, SparseCore 0:
  255.4 53.5 all-gather.2
  323.2 19.0 all-reduce.2
  352.7 19.1 all-reduce.4
where the time goes:
time: 386 us
  waiting for transfers between devices  238 us (62%)
  local copies, waits for them, and re-layouts  74.7 us (19%)
  matrix products  27 us (7%)
  blocking collectives  23 us (6%)
  between operations  13.3 us (3%)
  starting transfers between devices  4.86 us (1%)
  other arithmetic  4.48 us (1%)
    all_to_all x1, waiting for transfers between devices, on_device(): lax.all_to_all(item_table[lax.all_to_all(requests, 'users', split_axis=0,...  154 us
    all_gather x1, waiting for transfers between devices, on_device(): embedded = lax.all_gather(halves, 'cols', axis=1, tiled=True)  50.9 us
    gather x1, local copies, waits for them, and re-layouts, on_device(): item_table[lax.all_to_all(requests, 'users', split_axis=0, concat_axis=0,...  33.6 us
    psum x2, waiting for transfers between devices, on_device(): squares, dots = lax.psum((partial_value, products), 'cols')  33.4 us
    gather x1, local copies, waits for them, and re-layouts, on_device(): halves = answers.reshape(owners * capacity, half)[slot]  21.9 us
    scatter x1, local copies, waits for them, and re-layouts, on_device(): jnp.zeros((owners * capacity,), jnp.int32).at[slot].set(row_in)  15.5 us
    all_to_all x1, blocking collectives, on_device(): lax.all_to_all(requests, 'users', split_axis=0, concat_axis=0, tiled=True)  15.5 us
    dot_general x2, matrix products, on_device(): jnp.einsum('utd,ukd->utk', mapped, summed, preferred_element_type=jnp.flo...  10.2 us
  transfers between devices with their start and end apart: 4, of which 4 were waited for; matrix products, arithmetic and copies ran while one was open for 1% of the time, Pallas kernels for 0%

commit v1 on v0

v1 whole, which is shorter than its diff:
```python
import functools

import jax
import jax.numpy as jnp
from jax import lax
from jax.experimental import pallas as pl
from jax.experimental.pallas import tpu as pltpu
from jax.sharding import PartitionSpec as P

ITERS = 3
F32, BF16, I32 = jnp.float32, jnp.bfloat16, jnp.int32
NT = (((1,), (1,)), ((), ()))
VMEM = pl.BlockSpec(memory_space=pltpu.VMEM)
SMEM = pl.BlockSpec(memory_space=pltpu.SMEM)


def squash_scale(squares):
    return squares / (1.0 + squares) / jnp.sqrt(squares + 1e-06)


def div_mod(value, by):
    if by & (by - 1) == 0:
        return value >> (by.bit_length() - 1), value & (by - 1)
    quotient = lax.div(value, jnp.full(value.shape, by, I32))
    return quotient, value - quotient * by


def iota(shape, dim):
    return lax.broadcasted_iota(I32, shape, dim)


def dot(a, b):
    return jnp.dot(a, b, preferred_element_type=F32)


def dot_nt(a, b, **kw):
    return lax.dot_general(a, b, NT, preferred_element_type=F32, **kw)


def bits(mask):
    return jnp.where(mask, 1.0, 0.0).astype(BF16)


def pick(mask, value):
    return jnp.where(mask, value.astype(F32), 0.0).astype(BF16)


def positions(owner, owners):
    users, hist = owner.shape
    masks = jnp.concatenate([jnp.where(owner == s, 1.0, 0.0) for s in range(owners)], axis=0).astype(BF16)
    before = bits(iota((hist, hist), 0) < iota((hist, hist), 1))
    within = dot(masks, before)
    totals = dot(masks, jnp.ones((hist, hist), BF16))
    stacked = owners * users
    si, ui = div_mod(iota((stacked, stacked), 0), users)
    sj, uj = div_mod(iota((stacked, stacked), 1), users)
    earlier = dot(bits((si == sj) & (uj < ui)), totals.astype(BF16))
    rank = within + earlier
    pos = jnp.full(owner.shape, -1.0, F32)
    for s in range(owners):
        pos = jnp.where(owner == s, rank[s * users : (s + 1) * users], pos)
    return pos.astype(I32), masks


def prep_kernel(local_ref, ids_ref, seeds_ref, col_ref, row_ref, blocks_ref, dest_ref, *, owners, rows_dev, seeds, cap):
    users, hist = ids_ref.shape
    col, row = col_ref[...], row_ref[...]
    i, j = iota((users, users), 1), iota((users, users), 0)
    ahead = (row > col) | ((row == col) & (i < j))
    rank = jnp.sum(jnp.where(ahead, 1.0, 0.0), axis=1, keepdims=True).astype(I32)
    dest = div_mod(rank + local_ref[0], users)[1]
    dest_ref[...] = dest
    live = iota((users, hist), 1) < col
    packed = jnp.where(live, ids_ref[...] * seeds + seeds_ref[...], -1)
    place = iota((users, hist), 0)
    meta = jnp.full((users, hist), -1, I32)
    for j in range(users):
        meta = jnp.where(place == dest[j : j + 1, :], packed[j : j + 1, :], meta)
    ids = div_mod(meta, seeds)[0]
    owner, row_in = div_mod(ids, rows_dev)
    owner = jnp.where(meta >= 0, owner, -1)
    pos, masks = positions(owner, owners)
    lists = jnp.zeros((owners, cap), F32)
    slot = iota((cap, hist), 0)
    shard = iota((owners, hist), 0)
    for v in range(users):
        onehot = bits(slot == pos[v : v + 1, :])
        mine = shard == owner[v : v + 1, :]
        value = row_in[v : v + 1, :] + v * rows_dev
        low = value & 255
        lists = lists + dot_nt(pick(mine, low), onehot) + dot_nt(pick(mine, value - low), onehot)
    counts = dot_nt(jnp.ones((8, hist), BF16), masks)
    pairs = owners * users
    blocks_ref[:, :cap] = lists.astype(I32)
    blocks_ref[:, cap : cap + pairs] = jnp.broadcast_to(counts[:1].astype(I32), (owners, pairs))
    for group in range(owners // users):
        blocks_ref[group * users : (group + 1) * users, cap + pairs :] = meta


def owner_kernel(me_ref, recv_ref, mapped_ref, send_ref, index_ref, *, users, cap):
    v = pl.program_id(0)
    room = send_ref.shape[1]
    rows_dev = mapped_ref.shape[0]
    pairs = recv_ref.shape[0] * users
    local = lax.rem(v, users)

    @pl.when(local == 0)
    def _():
        got = recv_ref[pl.ds(pl.multiple_of(v, users), users), :]
        lists, counts = got[:, :cap], got[:, cap : cap + pairs].astype(F32).astype(BF16)
        s, w = div_mod(iota((pairs, 128), 0), users)
        lane = iota((pairs, 128), 1)
        here = s == me_ref[0]
        count = dot(counts, bits(here & (w == lane)))
        start = dot(counts, bits(here & (w < lane)))
        earlier = bits(iota((users, users), 1) < iota((users, users), 0))
        delta = (dot(earlier, count.astype(BF16)) - start).astype(I32)
        total = start[:, users : users + 1].astype(I32)
        rank = iota((users, cap), 1)
        valid = rank < total
        to, row = div_mod(lists, rows_dev)
        to = jnp.where(valid, to, -1)
        pos = rank
        for w in range(users):
            pos = pos + jnp.where(to == w, delta[:, w : w + 1], 0)
        pos = jnp.where(valid, pos, -1)
        slot = iota((room, cap), 0)
        shard = iota((users, cap), 0)
        index = jnp.zeros((room, users), F32)
        for u in range(users):
            onehot = bits(slot == pos[u : u + 1, :])
            mine = shard == to[u : u + 1, :]
            value = row[u : u + 1, :]
            low = value & 255
            index = index + dot_nt(onehot, pick(mine, low)) + dot_nt(onehot, pick(mine, value - low))
        index_ref[...] = index

    column = jnp.sum(jnp.where(iota(index_ref.shape, 1) == local, index_ref[...], 0.0), axis=1, keepdims=True)
    onehot = bits(iota((room, rows_dev), 1) == column.astype(I32))
    send_ref[0] = dot(onehot, mapped_ref[...]).astype(BF16)


def meta_kernel(meta_ref, seed_ref, user_ref, *, owners, rows_dev, seeds):
    users, hist = meta_ref.shape
    room = seed_ref.shape[1]
    meta = meta_ref[...]
    ids, seed = div_mod(meta, seeds)
    owner = jnp.where(meta >= 0, div_mod(ids, rows_dev)[0], -1)
    pos, _ = positions(owner, owners)
    slot = iota((room, hist), 0)
    shard = iota((owners, hist), 0)
    found = jnp.zeros((2 * owners, room), F32)
    for u in range(users):
        onehot = bits(slot == pos[u : u + 1, :])
        mine = shard == owner[u : u + 1, :]
        both = jnp.concatenate([jnp.where(mine, seed[u : u + 1, :].astype(F32), 0.0), jnp.where(mine, u + 1.0, 0.0)], axis=0)
        found = found + dot_nt(both.astype(BF16), onehot)
    seed_ref[...] = found[:owners].astype(I32)
    user_ref[...] = found[owners:].astype(I32)


def route(logits_of, rows_ref, user_ref, summed_ref, logits_ref):
    owners, room, half = rows_ref.shape
    lanes = summed_ref.shape[0]
    for s in range(owners):
        logits = logits_of(s)
        if logits_ref is not None:
            logits_ref[s] = logits
        caps = logits.shape[0]
        user = user_ref[s : s + 1, :]
        top = jnp.max(logits, axis=0, keepdims=True)
        raised = jnp.exp(logits - top)
        weights = raised / jnp.sum(raised, axis=0, keepdims=True)
        spread = jnp.concatenate([jnp.where(user == u + 1, weights, 0.0) for u in range(lanes // caps)], axis=0)
        part = dot(spread.astype(BF16), rows_ref[s])
        if s == 0:
            summed_ref[...] = part
        else:
            summed_ref[...] += part


def chosen(values, user, caps):
    total = jnp.zeros((caps, user.shape[1]), F32)
    for u in range(values.shape[0] // caps):
        total = jnp.where(user == u + 1, values[u * caps : (u + 1) * caps], total)
    return total


def products(rows_ref, user_ref, summed_ref, sent_ref, caps):
    owners, room, half = rows_ref.shape
    summed = summed_ref[...]
    lanes = summed.shape[0]
    high = summed.astype(BF16)
    low = (summed - high.astype(F32)).astype(BF16)
    both = jnp.concatenate([high, low], axis=0)
    for s in range(owners):
        dots = dot_nt(both, rows_ref[s])
        dots = dots[:lanes] + dots[lanes:]
        sent_ref[s * caps : (s + 1) * caps, :room] = chosen(dots, user_ref[s : s + 1, :], caps)
    sent_ref[:lanes, room:] = jnp.broadcast_to(
        jnp.sum(summed * summed, axis=1, keepdims=True), (lanes, sent_ref.shape[1] - room)
    )
    if sent_ref.shape[0] > lanes:
        sent_ref[lanes:, room:] = jnp.zeros((sent_ref.shape[0] - lanes, sent_ref.shape[1] - room), F32)


def first_kernel(rows_ref, seed_ref, user_ref, table_ref, logits_ref, sent_ref, summed_ref):
    caps, seeds = table_ref.shape
    room = rows_ref.shape[1]

    def initial(s):
        onehot = jnp.where(iota((seeds, room), 0) == seed_ref[s : s + 1, :], 1.0, 0.0)
        return jnp.dot(table_ref[...], onehot, precision=lax.Precision.HIGHEST, preferred_element_type=F32)

    route(initial, rows_ref, user_ref, summed_ref, logits_ref)
    products(rows_ref, user_ref, summed_ref, sent_ref, caps)


def later_kernel(*refs, cols, last, lanes):
    parts, (rows_ref, user_ref, old_ref), outs = refs[:cols], refs[cols : cols + 3], refs[cols + 3 :]
    owners, room, half = rows_ref.shape
    caps = old_ref.shape[1]
    squares = sum(part[:lanes, room : room + 1] for part in parts)
    scale = squash_scale(squares)

    def updated(s):
        dots = sum(part[s * caps : (s + 1) * caps, :room] for part in parts)
        user = user_ref[s : s + 1, :]
        wide = jnp.broadcast_to(scale, (lanes, room))
        return old_ref[s] + dots * chosen(wide, user, caps)

    if last:
        summed_ref, square_ref = outs
        route(updated, rows_ref, user_ref, summed_ref, None)
        summed = summed_ref[...]
        square_ref[...] = jnp.broadcast_to(jnp.sum(summed * summed, axis=1, keepdims=True), square_ref.shape)
    else:
        logits_ref, sent_ref, summed_ref = outs
        route(updated, rows_ref, user_ref, summed_ref, logits_ref)
        products(rows_ref, user_ref, summed_ref, sent_ref, caps)


def call(kernel, out_shape, n_in, smem=(), **kw):
    ins = [SMEM if i in smem else VMEM for i in range(n_in)]
    return pl.pallas_call(kernel, out_shape=out_shape, in_specs=ins, out_specs=jax.tree.map(lambda _: VMEM, out_shape), **kw)


def shifted(x, by):
    cols = lax.axis_size("cols")
    return lax.ppermute(x, "cols", [((i + by) % cols, i) for i in range(cols)])


def all_cols(x):
    return [x] + [shifted(x, by) for by in range(1, lax.axis_size("cols"))]


def map_table(item_table, bilinear):
    cols = lax.axis_size("cols")
    mine = lax.axis_index("cols")
    width = item_table.shape[1]
    total = None
    for by, part in enumerate(all_cols(item_table)):
        at = lax.rem(mine + by, cols) * width
        factor = lax.dynamic_slice_in_dim(bilinear, at, width, 0)
        term = dot(part, factor)
        total = term if total is None else total + term
    return total.astype(BF16)


def owner_ranks(owner, owners):
    tok_count = owner.shape[0]
    span = min(256, tok_count)
    onehot = (owner[:, None] == jnp.arange(owners, dtype=I32)[None, :]).astype(F32)
    blocked = onehot.reshape(tok_count // span, span, owners)
    lower = (iota((span, span), 0) >= iota((span, span), 1)).astype(F32)
    within = jnp.einsum("ij,bjo->bio", lower, blocked)
    totals = within[:, -1, :]
    before = jnp.cumsum(totals, axis=0) - totals
    counts = (within + before[:, None, :]).reshape(tok_count, owners)
    return (jnp.sum(counts * onehot, axis=1) - 1.0).astype(I32)


def any_input(item_ids, lengths, seed_rows, mapped_rows, seed_table, cap):
    users_here, hist = item_ids.shape
    owners = lax.axis_size("users")
    rows_dev, half = mapped_rows.shape
    tok_count = users_here * hist
    flat_ids = item_ids.reshape(tok_count)
    owner = flat_ids // rows_dev
    slot = owner * cap + owner_ranks(owner, owners)
    requests = jnp.zeros((owners * cap,), I32).at[slot].set(flat_ids % rows_dev).reshape(owners, cap)
    asked = lax.all_to_all(requests, "users", split_axis=0, concat_axis=0, tiled=True)
    answers = lax.all_to_all(mapped_rows[asked], "users", split_axis=0, concat_axis=0, tiled=True)
    mapped = answers.reshape(owners * cap, half)[slot].reshape(users_here, hist, half)
    logits = seed_table[seed_rows]
    live = (jnp.arange(hist, dtype=I32)[None, :] < lengths[:, None]).astype(F32)
    for step in range(ITERS):
        weights = (jax.nn.softmax(logits, axis=-1) * live[:, :, None]).astype(BF16)
        summed = jnp.einsum("utk,utd->ukd", weights, mapped, preferred_element_type=F32)
        squares = sum(all_cols(jnp.sum(summed * summed, axis=-1)))
        scale = squash_scale(squares)
        if step + 1 < ITERS:
            dots = jnp.einsum(
                "utd,ukd->utk", mapped, summed, preferred_element_type=F32, precision=lax.Precision.HIGHEST
            )
            logits = logits + sum(all_cols(dots)) * scale[:, None, :]
    return summed * scale[:, :, None]


def on_device(item_ids, lengths, seed_rows, item_table, bilinear, seed_table):
    users, hist = item_ids.shape
    owners = lax.axis_size("users")
    cols = lax.axis_size("cols")
    me = lax.axis_index("users")
    rows_dev = item_table.shape[0]
    half = bilinear.shape[1]
    seeds, caps = seed_table.shape
    tok_count = users * hist
    cap = max(2, (2 * tok_count + owners - 1) // owners)
    room = -(-cap * 7 // 16 // 16) * 16
    pairs = owners * users
    lanes = users * caps
    assert owners % users == 0 and hist <= 256 and seeds <= 256 and rows_dev * users <= 65536
    local = lax.rem(me, users)
    group = me - local

    mapped_rows = map_table(item_table, bilinear)
    blocks, dest = call(
        functools.partial(prep_kernel, owners=owners, rows_dev=rows_dev, seeds=seeds, cap=cap),
        (jax.ShapeDtypeStruct((owners, cap + pairs + hist), I32), jax.ShapeDtypeStruct((users, 1), I32)),
        5,
        smem=(0,),
    )(local.reshape(1), item_ids, seed_rows, lengths.reshape(users, 1), lengths.reshape(1, users))
    recv = lax.all_to_all(blocks, "users", split_axis=0, concat_axis=0, tiled=True)
    counts = recv[:, cap : cap + pairs].reshape(owners // users, users, pairs)
    fits = jnp.max(jnp.sum(counts, axis=1)) <= room

    def dealt(recv, mapped_rows, dest, seed_table, *_):
        width = recv.shape[1]
        send = pl.pallas_call(
            functools.partial(owner_kernel, users=users, cap=cap),
            grid=(owners,),
            out_shape=jax.ShapeDtypeStruct((owners, room, half), BF16),
            in_specs=[
                SMEM,
                pl.BlockSpec((owners, width), lambda v: (0, 0)),
                pl.BlockSpec((rows_dev, half), lambda v: (0, 0)),
            ],
            out_specs=pl.BlockSpec((1, room, half), lambda v: (v, 0, 0)),
            scratch_shapes=[pltpu.VMEM((room, users), F32)],
        )(me.reshape(1), recv, mapped_rows)
        rows = lax.all_to_all(send, "users", split_axis=0, concat_axis=0, tiled=True)
        meta = lax.dynamic_slice(recv, (group, cap + pairs), (users, hist))
        where = jax.ShapeDtypeStruct((owners, room), I32)
        seed, user = call(
            functools.partial(meta_kernel, owners=owners, rows_dev=rows_dev, seeds=seeds), (where, where), 1
        )(meta)
        logits_shape = jax.ShapeDtypeStruct((owners, caps, room), F32)
        wide = (room // 128 + 1) * 128
        sent_shape = jax.ShapeDtypeStruct((owners * caps, wide), F32)
        summed_shape = jax.ShapeDtypeStruct((lanes, half), F32)
        square_shape = jax.ShapeDtypeStruct((lanes, 128), F32)
        step_shapes = (logits_shape, sent_shape, summed_shape)
        logits, sent, _ = call(first_kernel, step_shapes, 4)(rows, seed, user, seed_table.T)
        for _ in range(ITERS - 2):
            kernel = functools.partial(later_kernel, cols=cols, last=False, lanes=lanes)
            logits, sent, _ = call(kernel, step_shapes, cols + 3)(*all_cols(sent), rows, user, logits)
        kernel = functools.partial(later_kernel, cols=cols, last=True, lanes=lanes)
        summed, square = call(kernel, (summed_shape, square_shape), cols + 3)(*all_cols(sent), rows, user, logits)
        scale = squash_scale(sum(all_cols(square))[:, :1])
        capsules = (summed * scale).reshape(users, caps, half)
        if owners > users:
            spread = jnp.zeros((owners, caps, half), F32)
            capsules = lax.dynamic_update_slice_in_dim(spread, capsules, group, 0)
        back = lax.all_to_all(capsules, "users", split_axis=0, concat_axis=0, tiled=True)
        if owners > users:
            back = lax.dynamic_slice_in_dim(back, group, users, 0)
        return back[dest[:, 0]]

    def full(recv, mapped_rows, dest, seed_table, item_ids, lengths, seed_rows):
        return any_input(item_ids, lengths, seed_rows, mapped_rows, seed_table, cap)

    return lax.cond(fits, dealt, full, recv, mapped_rows, dest, seed_table, item_ids, lengths, seed_rows)


def solution(mesh):
    placed = (
        P("users", None),
        P("users"),
        P("users", None),
        P("users", "cols"),
        P(None, "cols"),
        P(),
    )
    return jax.shard_map(
        on_device, mesh=mesh, in_specs=placed, out_specs=P("users", None, "cols"), check_vma=False
    )
```

time: 386 us -> 177 us (0.46)
  waiting for transfers between devices: 238 us -> 83.8 us
  local copies, waits for them, and re-layouts: 74.7 us -> 10.1 us
  Pallas kernels: 0 us -> 37.4 us
  starting transfers between devices: 4.86 us -> 30.7 us
  blocking collectives: 23 us -> 0 us
  matrix products: 27 us -> 9.69 us
  between operations: 13.3 us -> 0.76 us
    all_to_all x1 -> x3, waiting for transfers between devices: 154 us -> 79.5 us  [the longest x1 66.7 us: dealt(): lax.all_to_all(send, 'users', split_axis=0, concat_axis=0, tiled=True)]
    gather x2 -> x1, local copies, waits for them, and re-layouts: 55.4 us -> 0.56 us  [dealt(): return back[dest[:, 0]]]
    all_gather x1 -> x0, waiting for transfers between devices: 50.9 us -> none  [on_device(): embedded = lax.all_gather(halves, 'cols', axis=1, tiled=True)]
    pallas_call x0 -> x6, Pallas kernels: none -> 37.4 us  [the longest x1 16.1 us: dealt(): pl.pallas_call(functools.partial(owner_kernel, users=users, cap=cap), gri...]
    psum x2 -> x0, waiting for transfers between devices: 33.4 us -> none  [on_device(): squares, dots = lax.psum((partial_value, products), 'cols')]
    all_to_all x1 -> x3, starting transfers between devices: 4.74 us -> 29.9 us  [the longest x1 17.5 us: dealt(): lax.all_to_all(capsules, 'users', split_axis=0, concat_axis=0, tiled=True)]
    dot_general x8 -> x2, matrix products: 27 us -> 9.69 us  [dot(): return jnp.dot(a, b, preferred_element_type=F32)]
    scatter x1 -> x0, local copies, waits for them, and re-layouts: 15.5 us -> none  [on_device(): jnp.zeros((owners * capacity,), jnp.int32).at[slot].set(row_in)]
  transfers between devices with their start and end apart: 4 -> 7, of which waited for: 4 -> 6; matrix products, arithmetic and copies ran while one was open for 1% -> 5% of each run, Pallas kernels for 0% -> 4%
where the time goes in v1:
time: 177 us; the launch traced here: 176 us
  waiting for transfers between devices  83.8 us (47%)
  Pallas kernels  37.4 us (21%)
  starting transfers between devices  30.7 us (17%)
  local copies, waits for them, and re-layouts  10.1 us (6%)
  matrix products  9.69 us (5%)
  other arithmetic  3.36 us (2%)
    all_to_all x1, waiting for transfers between devices, dealt(): lax.all_to_all(send, 'users', split_axis=0, concat_axis=0, tiled=True)  66.7 us
    all_to_all x1, starting transfers between devices, dealt(): lax.all_to_all(capsules, 'users', split_axis=0, concat_axis=0, tiled=True)  17.5 us
    pallas_call x1, Pallas kernels, dealt(): pl.pallas_call(functools.partial(owner_kernel, users=users, cap=cap), gri...  16.1 us
    all_to_all x1, waiting for transfers between devices, dealt(): lax.all_to_all(capsules, 'users', split_axis=0, concat_axis=0, tiled=True)  10.1 us
    dot_general x2, matrix products, dot(): return jnp.dot(a, b, preferred_element_type=F32)  9.69 us
    all_to_all x1, starting transfers between devices, on_device(): lax.all_to_all(blocks, 'users', split_axis=0, concat_axis=0, tiled=True)  7.95 us
    pallas_call x1, Pallas kernels, dealt(): call(first_kernel, step_shapes, 4)(rows, seed, user, seed_table.T)  5.51 us
    pallas_call x1, Pallas kernels, dealt(): call(kernel, step_shapes, cols + 3)(*all_cols(sent), rows, user, logits)  5.13 us
  transfers between devices with their start and end apart: 7, of which 6 were waited for; matrix products, arithmetic and copies ran while one was open for 5% of the time, Pallas kernels for 4%

profile of v1, /device:TPU:0, one launch (start us, length us, event | category | flops | bytes accessed | tf_op | source)
XLA Modules:
  0.0 176.1 jit_solution(15162158051179315691)
XLA Ops:
  0.0 0.5 collective-permute-start.8
  0.5 1.3 copy.37.col_ref
  1.8 4.3 %shard_map.66 = (s32[16,1024]{1,0:T(8,128)}, s32[16,1]{1,0:T(8,128)S(1)}) custom-call(s32[1]{0:T(128)} %bitcast.14.local_ref, s32[16,256]{1,0:T(8,128)} %ids_ref.1, s32[16,256]{1,0:T(8,128)} %seeds_ref.1, s32[16,1]{1,0:T(8,128)} %copy.37.col_ref, s32[1,16]{1,0:T(1,128)} %bitcast.80), custom_call_target="tpu_custom_call" | custom-call | tf_op jit(solution)/shard_map/pallas_call | solution.py:328
  6.2 1.5 copy.38
  7.7 7.9 %all-to-all-start.4 = ((s32[16,1,1024]{2,1,0:T(1,128)}), s32[16,1,1024]{2,1,0:T(1,128)S(1)}, u32[]{:S(2)}, u32[]{:S(2)}) async-start(s32[16,1,1024]{2,1,0:T(1,128)} %copy.38), calls=%async_computation.4 | async-start | bytes 131072 | tf_op jit(solution)/shard_map/all_to_all | solution.py:334
  15.7 4.8 %fusion.35 = f32[512,2048]{1,0:T(8,128)} fusion(bf16[2048,512]{1,0:T(8,128)(2,1)} %param.11, bf16[1024,512]{1,0:T(8,128)(2,1)S(1)} %copy-done, s32[]{:T(128)S(6)} %select_n.59), kind=kOutput, calls=%fused_computation.83 | convolution fusion | flops 1073741824 | bytes 6815748 | tf_op jit(solution)/shard_map/dot_general | solution.py:33
  20.5 2.7 %all-to-all-done.4 = s32[16,1,1024]{2,1,0:T(1,128)S(1)} async-done(((s32[16,1,1024]{2,1,0:T(1,128)}), s32[16,1,1024]{2,1,0:T(1,128)S(1)}, u32[]{:S(2)}, u32[]{:S(2)}) %all-to-all-start.4) | async-done | bytes 65568 | tf_op jit(solution)/shard_map/all_to_all | solution.py:334
  23.2 0.6 reduce_max.36
  24.6 4.9 %fusion.33 = bf16[2048,512]{0,1:T(8,128)(2,1)} fusion(f32[512,2048]{1,0:T(8,128)} %fusion.35, bf16[2048,512]{1,0:T(8,128)(2,1)S(1)} %collective-permute-done.8, bf16[1024,512]{1,0:T(8,128)(2,1)S(1)} %copy-done, s32[]{:T(128)S(6)} %select_n.60), kind=kOutput, calls=%fused_computation.81 | convolution fusion | flops 1075838976 | bytes 8912900 | tf_op jit(solution)/shard_map/dot_general | solution.py:33
  29.5 145.9 %conditional.1 = (f32[16,8,512]{2,1,0:T(8,128)S(1)}) conditional(s32[]{:T(128)} %convert_element_type.40, (s32[16,256]{1,0:T(8,128)S(1)}, f32[64,8]{0,1:T(8,128)S(1)}, s32[16,256]{1,0:T(8,128)S(1)}, bf16[2048,512]{0,1:T(8,128)(2,1)}, s32[16]{0:T(128)S(1)}) %tuple.34, (s32[]{:T(128)}, s32[16,1024]{1,0:T(8,128)S(1)}, bf16[2048,512]{0,1:T(8,128)(2,1)}, ...), branch_computations={%region_2.15_spmd, %region_15.16_spmd} | conditional | flops 538801664 | bytes 99465072 | solution.py:383
  29.7 3.9 %copy.41.mapped_ref = bf16[2048,512]{1,0:T(8,128)(2,1)} copy(bf16[2048,512]{0,1:T(8,128)(2,1)} %get-tuple-element.89) | data formatting | bytes 4194304 | tf_op jit(solution)/shard_map
  33.6 16.1 %branch_1_fun.5 = bf16[16,224,512]{2,1,0:T(8,128)(2,1)} custom-call(s32[1]{0:T(128)} %bitcast.10.me_ref, s32[16,1024]{1,0:T(8,128)S(1)} %get-tuple-element.35.recv_ref, bf16[2048,512]{1,0:T(8,128)(2,1)} %copy.41.mapped_ref), custom_call_target="tpu_custom_call" | custom-call | tf_op jit(solution)/shard_map/cond/branch_1_fun/pallas_call | solution.py:340
  49.8 4.5 %all-to-all-start = ((bf16[16,224,512]{2,1,0:T(8,128)(2,1)}), bf16[16,224,512]{2,1,0:T(8,128)(2,1)}, u32[]{:S(2)}, u32[]{:S(2)}) async-start(bf16[16,224,512]{2,1,0:T(8,128)(2,1)} %branch_1_fun.5), calls=%async_computation | async-start | bytes 7340032 | tf_op jit(solution)/shard_map/cond/branch_1_fun/all_to_all | solution.py:352
  54.3 0.6 dynamic_slice.6.meta_ref
  54.9 2.5 %branch_1_fun.6 = (s32[16,224]{1,0:T(8,128)}, s32[16,224]{1,0:T(8,128)}) custom-call(s32[16,256]{1,0:T(8,128)} %dynamic_slice.6.meta_ref), custom_call_target="tpu_custom_call" | custom-call | tf_op jit(solution)/shard_map/cond/branch_1_fun/pallas_call | solution.py:355
  57.4 66.7 %all-to-all-done.rows_ref.refs_2_ = bf16[16,224,512]{2,1,0:T(8,128)(2,1)} async-done(((bf16[16,224,512]{2,1,0:T(8,128)(2,1)}), bf16[16,224,512]{2,1,0:T(8,128)(2,1)}, u32[]{:S(2)}, u32[]{:S(2)}) %all-to-all-start) | async-done | bytes 3670048 | tf_op jit(solution)/shard_map/cond/branch_1_fun/all_to_all | solution.py:352
  124.1 5.5 %branch_1_fun.7 = (f32[16,8,224]{2,1,0:T(8,128)}, f32[128,256]{1,0:T(8,128)}, f32[128,512]{1,0:T(8,128)}) custom-call(bf16[16,224,512]{2,1,0:T(8,128)(2,1)} %all-to-all-done.rows_ref.refs_2_, s32[16,224]{1,0:T(8,128)} %get-tuple-element.37.seed_ref, s32[16,224]{1,0:T(8,128)} %get-tuple-element.38.user_ref.refs_3_, f32[8,64]{1,0:T(8,128)S(1)} %bitcast.78), custom_call_target="tpu_custom_call" | custom-call | tf_op jit(solution)/shard_map/cond/branch_1_fun/pallas_call | solution.py:364
  129.6 1.6 collective-permute-done.refs_1_
  131.2 0.6 copy-done.5
  131.8 5.1 %branch_1_fun.8 = (f32[16,8,224]{2,1,0:T(8,128)}, f32[128,256]{1,0:T(8,128)}, f32[128,512]{1,0:T(8,128)}) custom-call(f32[128,256]{1,0:T(8,128)} %get-tuple-element.40.refs_0_, f32[128,256]{1,0:T(8,128)} %copy-done.5, bf16[16,224,512]{2,1,0:T(8,128)(2,1)} %all-to-all-done.rows_ref.refs_2_, s32[16,224]{1,0:T(8,128)} %get-tuple-element.38.user_ref.refs_3_, ...), custom_call_target="tpu_custom_call" | custom-call | tf_op jit(solution)/shard_map/cond/branch_1_fun/pallas_call | solution.py:367
  136.9 0.1 collective-permute-start.1
  137.1 1.4 collective-permute-done.1.refs_1_
  138.5 0.6 copy-done.4
  139.1 3.8 %branch_1_fun.9 = (f32[128,512]{1,0:T(8,128)}, f32[128,128]{1,0:T(8,128)}) custom-call(f32[128,256]{1,0:T(8,128)} %get-tuple-element.42.refs_0_, f32[128,256]{1,0:T(8,128)} %copy-done.4, bf16[16,224,512]{2,1,0:T(8,128)(2,1)} %all-to-all-done.rows_ref.refs_2_, s32[16,224]{1,0:T(8,128)} %get-tuple-element.38.user_ref.refs_3_, ...), custom_call_target="tpu_custom_call" | custom-call | tf_op jit(solution)/shard_map/cond/branch_1_fun/pallas_call | solution.py:369
  142.9 0.1 collective-permute-start.2
  143.1 1.3 collective-permute-done.2
  144.4 1.0 fusion.1
  145.4 1.7 multiply_bitcast_fusion
  147.1 17.5 %all-to-all-start.1 = ((f32[16,8,512]{2,1,0:T(8,128)}), f32[16,8,512]{2,1,0:T(8,128)S(1)}, u32[]{:S(2)}, u32[]{:S(2)}) async-start(f32[16,8,512]{2,1,0:T(8,128)} %multiply_bitcast_fusion), calls=%async_computation.1 | async-start | bytes 524288 | tf_op jit(solution)/shard_map/cond/branch_1_fun/all_to_all | solution.py:375
  164.7 10.1 %all-to-all-done.1 = f32[16,8,512]{2,1,0:T(8,128)S(1)} async-done(((f32[16,8,512]{2,1,0:T(8,128)}), f32[16,8,512]{2,1,0:T(8,128)S(1)}, u32[]{:S(2)}, u32[]{:S(2)}) %all-to-all-start.1) | async-done | bytes 262176 | tf_op jit(solution)/shard_map/cond/branch_1_fun/all_to_all | solution.py:375
  174.8 0.6 gather_fusion
  175.4 0.7 copy-done.2
  (20 shorter events, 0.2 us)
Async XLA Ops:
  0.0 15.7 %copy-start = (bf16[1024,512]{1,0:T(8,128)(2,1)S(1)}, bf16[1024,512]{1,0:T(8,128)(2,1)}, u32[]{:S(2)}) copy-start(bf16[1024,512]{1,0:T(8,128)(2,1)} %param.12) | copy-start | bytes 3145732
  0.0 24.6 %collective-permute-start.8 = (bf16[2048,512]{1,0:T(8,128)(2,1)}, bf16[2048,512]{1,0:T(8,128)(2,1)S(1)}, u32[]{:S(2)}, u32[]{:S(2)}) collective-permute-start(bf16[2048,512]{1,0:T(8,128)(2,1)} %param.11), channel_id=1, source_target_pairs={{1,0},{0,1},{3,2},{2,3},{5,4},{4,5},{7,6},{6,7},{9,8},{8,9},{11,10... | collective-permute-start | bytes 6291464 | tf_op jit(solution)/shard_map/ppermute | solution.py:250
  7.7 15.5 %all-to-all-start.4 = ((s32[16,1,1024]{2,1,0:T(1,128)}), s32[16,1,1024]{2,1,0:T(1,128)S(1)}, u32[]{:S(2)}, u32[]{:S(2)}) async-start(s32[16,1,1024]{2,1,0:T(1,128)} %copy.38), calls=%async_computation.4 | async-start | bytes 131072 | tf_op jit(solution)/shard_map/all_to_all | solution.py:334
  24.5 4.9 %copy-start.3 = (s32[16,256]{1,0:T(8,128)S(1)}, s32[16,256]{1,0:T(8,128)}, u32[]{:S(2)}) copy-start(s32[16,256]{1,0:T(8,128)} %ids_ref.1) | copy-start | bytes 49156
  24.5 4.9 %copy-start.6 = (s32[16,256]{1,0:T(8,128)S(1)}, s32[16,256]{1,0:T(8,128)}, u32[]{:S(2)}) copy-start(s32[16,256]{1,0:T(8,128)} %seeds_ref.1) | copy-start | bytes 49156
  24.5 4.9 %copy-start.7 = (f32[64,8]{0,1:T(8,128)S(1)}, f32[64,8]{0,1:T(8,128)}, u32[]{:S(2)}) copy-start(f32[64,8]{0,1:T(8,128)} %param.13) | copy-start | bytes 6148
  24.5 4.9 %copy-start.8 = (s32[16]{0:T(128)S(1)}, s32[16]{0:T(128)}, u32[]{:S(2)}) copy-start(s32[16]{0:T(128)} %param.9) | copy-start | bytes 196
  49.8 74.3 %all-to-all-start = ((bf16[16,224,512]{2,1,0:T(8,128)(2,1)}), bf16[16,224,512]{2,1,0:T(8,128)(2,1)}, u32[]{:S(2)}, u32[]{:S(2)}) async-start(bf16[16,224,512]{2,1,0:T(8,128)(2,1)} %branch_1_fun.5), calls=%async_computation | async-start | bytes 7340032 | tf_op jit(solution)/shard_map/cond/branch_1_fun/all_to_all | solution.py:352
  129.6 1.6 collective-permute-start
  131.2 0.6 copy-start.5
  136.9 1.6 collective-permute-start.1
  138.5 0.6 copy-start.4
  142.9 1.5 collective-permute-start.2
  147.1 27.7 %all-to-all-start.1 = ((f32[16,8,512]{2,1,0:T(8,128)}), f32[16,8,512]{2,1,0:T(8,128)S(1)}, u32[]{:S(2)}, u32[]{:S(2)}) async-start(f32[16,8,512]{2,1,0:T(8,128)} %multiply_bitcast_fusion), calls=%async_computation.1 | async-start | bytes 524288 | tf_op jit(solution)/shard_map/cond/branch_1_fun/all_to_all | solution.py:375
  175.4 0.7 copy-start.2

commit v2 on v1

v2 whole, which is shorter than its diff:
```python
import functools
import math

import jax
import jax.numpy as jnp
from jax import lax
from jax.experimental import pallas as pl
from jax.experimental.pallas import tpu as pltpu
from jax.sharding import PartitionSpec as P


ITERS = 3
F32, BF16, I32 = jnp.float32, jnp.bfloat16, jnp.int32
NT = (((1,), (1,)), ((), ()))
VMEM = pl.BlockSpec(memory_space=pltpu.VMEM)
SMEM = pl.BlockSpec(memory_space=pltpu.SMEM)


def squash_scale(squares):
    return squares / (1.0 + squares) / jnp.sqrt(squares + 1e-06)


def div_mod(value, by):
    if by & (by - 1) == 0:
        return value >> (by.bit_length() - 1), value & (by - 1)
    quotient = lax.div(value, jnp.full(value.shape, by, I32))
    return quotient, value - quotient * by


def iota(shape, dim):
    return lax.broadcasted_iota(I32, shape, dim)


def dot(a, b):
    return jnp.dot(a, b, preferred_element_type=F32)


def dot_nt(a, b, **kw):
    return lax.dot_general(a, b, NT, preferred_element_type=F32, **kw)


def bits(mask):
    return jnp.where(mask, 1.0, 0.0).astype(BF16)


def halves(mask, value):
    low = value & 255
    both = [jnp.where(mask, term.astype(F32), 0.0) for term in (low, value - low)]
    return jnp.concatenate(both, axis=0).astype(BF16)


def positions(owner, owners):
    users, hist = owner.shape
    masks = jnp.concatenate([jnp.where(owner == s, 1.0, 0.0) for s in range(owners)], axis=0).astype(BF16)
    before = bits(iota((hist, hist), 0) < iota((hist, hist), 1))
    within = dot(masks, before)
    totals = dot(masks, jnp.ones((hist, hist), BF16))
    stacked = owners * users
    si, ui = div_mod(iota((stacked, stacked), 0), users)
    sj, uj = div_mod(iota((stacked, stacked), 1), users)
    earlier = dot(bits((si == sj) & (uj < ui)), totals.astype(BF16))
    rank = within + earlier
    pos = jnp.full(owner.shape, -1.0, F32)
    for s in range(owners):
        pos = jnp.where(owner == s, rank[s * users : (s + 1) * users], pos)
    return pos.astype(I32), masks


def prep_kernel(local_ref, ids_ref, seeds_ref, row_ref, blocks_ref, dest_ref, *, owners, rows_dev, seeds, cap):
    users, hist = ids_ref.shape
    row = row_ref[...]
    i, j = iota((users, users), 1), iota((users, users), 0)
    col = jnp.sum(jnp.where(i == j, row.astype(F32), 0.0), axis=1, keepdims=True).astype(I32)
    ahead = (row > col) | ((row == col) & (i < j))
    rank = jnp.sum(jnp.where(ahead, 1.0, 0.0), axis=1, keepdims=True).astype(I32)
    dest = div_mod(rank + local_ref[0], users)[1]
    dest_ref[...] = dest
    live = iota((users, hist), 1) < col
    packed = jnp.where(live, ids_ref[...] * seeds + seeds_ref[...], -1)
    place = iota((users, hist), 0)
    meta = jnp.full((users, hist), -1, I32)
    for j in range(users):
        meta = jnp.where(place == dest[j : j + 1, :], packed[j : j + 1, :], meta)
    ids = div_mod(meta, seeds)[0]
    owner, row_in = div_mod(ids, rows_dev)
    owner = jnp.where(meta >= 0, owner, -1)
    pos, masks = positions(owner, owners)
    lists = jnp.zeros((2 * owners, cap), F32)
    slot = iota((cap, hist), 0)
    shard = iota((owners, hist), 0)
    for v in range(users):
        onehot = bits(slot == pos[v : v + 1, :])
        mine = shard == owner[v : v + 1, :]
        lists = lists + dot_nt(halves(mine, row_in[v : v + 1, :] + v * rows_dev), onehot)
    lists = lists[:owners] + lists[owners:]
    counts = dot_nt(jnp.ones((8, hist), BF16), masks)
    pairs = owners * users
    blocks_ref[:, 0, :cap] = lists.astype(I32)
    blocks_ref[:, 0, cap : cap + pairs] = jnp.broadcast_to(counts[:1].astype(I32), (owners, pairs))
    for group in range(owners // users):
        blocks_ref[group * users : (group + 1) * users, 0, cap + pairs :] = meta


def map_kernel(*refs, cols):
    at_ref, factor_ref, parts, (out_ref,) = refs[0], refs[1], refs[2 : 2 + cols], refs[2 + cols :]
    rows, width = parts[0].shape
    tall = min(256, rows)

    def one(i, carry):
        here = pl.ds(pl.multiple_of(i * tall, tall), tall)
        total = None
        for by, part in enumerate(parts):
            at = pl.multiple_of(lax.rem(at_ref[0] + by, cols) * width, width)
            term = dot(part[here, :], factor_ref[pl.ds(at, width), :])
            total = term if total is None else total + term
        out_ref[here, :] = total.astype(BF16)
        return carry

    lax.fori_loop(0, rows // tall, one, 0)


def gather_rows(index, mapped_ref, loc):
    column = jnp.sum(jnp.where(iota(index.shape, 1) == loc, index, 0.0), axis=1, keepdims=True)
    onehot = bits(iota((index.shape[0], mapped_ref.shape[0]), 1) == column.astype(I32))
    return dot(onehot, mapped_ref[...]).astype(BF16)


def index_of(me, got, owners, cap, room, rows_dev):
    users = got.shape[0]
    pairs = owners * users
    lists, counts = got[:, :cap], got[:, cap : cap + pairs].astype(F32).astype(BF16)
    s, w = div_mod(iota((pairs, 128), 0), users)
    lane = iota((pairs, 128), 1)
    here = s == me
    count = dot(counts, bits(here & (w == lane)))
    start = dot(counts, bits(here & (w < lane)))
    earlier = bits(iota((users, users), 1) < iota((users, users), 0))
    delta = (dot(earlier, count.astype(BF16)) - start).astype(I32)
    total = start[:, users : users + 1].astype(I32)
    rank = iota((users, cap), 1)
    valid = rank < total
    to, row = div_mod(lists, rows_dev)
    to = jnp.where(valid, to, -1)
    pos = rank
    for w in range(users):
        pos = pos + jnp.where(to == w, delta[:, w : w + 1], 0)
    pos = jnp.where(valid, pos, -1)
    slot = iota((room, cap), 0)
    shard = iota((users, cap), 0)
    index = jnp.zeros((room, 2 * users), F32)
    for u in range(users):
        onehot = bits(slot == pos[u : u + 1, :])
        mine = shard == to[u : u + 1, :]
        index = index + dot_nt(onehot, halves(mine, row[u : u + 1, :]))
    return index[:, :users] + index[:, users:]


def send_blocks(me, index_ref, mapped_ref, outs, block_ref, first):
    users = index_ref.shape[2]

    def one(i, carry):
        group, loc = div_mod(me ^ (first + i), users)
        block_ref[...] = gather_rows(index_ref[group], mapped_ref, loc)
        for k, out_ref in enumerate(outs):
            @pl.when(i == k)
            def _(out_ref=out_ref):
                out_ref[...] = block_ref[...]
        return carry

    lax.fori_loop(0, len(outs), one, 0)


def index_kernel(me_ref, recv_ref, mapped_ref, index_ref, *refs, first, cap):
    groups, room, users = index_ref.shape
    for g in range(groups):
        got = recv_ref[g * users : (g + 1) * users, 0, :]
        index_ref[g] = index_of(me_ref[0], got, recv_ref.shape[0], cap, room, mapped_ref.shape[0])
    send_blocks(me_ref[0], index_ref, mapped_ref, refs[:-1], refs[-1], first)


def gather_kernel(me_ref, index_ref, mapped_ref, after_ref, order_ref, *refs, first):
    send_blocks(me_ref[0], index_ref, mapped_ref, refs[:-1], refs[-1], first)
    order_ref[...] = jnp.zeros(order_ref.shape, F32)


def meta_kernel(me_ref, recv_ref, seed_ref, user_ref, *, users, hist, rows_dev, seeds):
    owners, room = seed_ref.shape
    group = pl.multiple_of(div_mod(me_ref[0], users)[0] * users, users)
    meta = recv_ref[pl.ds(group, users), 0, recv_ref.shape[2] - hist :]
    ids, seed = div_mod(meta, seeds)
    owner = jnp.where(meta >= 0, div_mod(ids, rows_dev)[0] ^ me_ref[0], -1)
    pos, _ = positions(owner, owners)
    slot = iota((room, hist), 0)
    shard = iota((owners, hist), 0)
    found = jnp.zeros((2 * owners, room), F32)
    for u in range(users):
        onehot = bits(slot == pos[u : u + 1, :])
        mine = shard == owner[u : u + 1, :]
        both = jnp.concatenate([jnp.where(mine, seed[u : u + 1, :].astype(F32), 0.0), jnp.where(mine, u + 1.0, 0.0)], axis=0)
        found = found + dot_nt(both.astype(BF16), onehot)
    seed_ref[...] = found[:owners].astype(I32)
    user_ref[...] = found[owners:].astype(I32)


def route(logits_of, rows_refs, user_ref, summed_ref, logits_ref):
    owners = len(rows_refs)
    lanes = summed_ref.shape[0]
    for s in range(owners):
        logits = logits_of(s)
        if logits_ref is not None:
            logits_ref[s] = logits
        caps = logits.shape[0]
        user = user_ref[s : s + 1, :]
        top = jnp.max(logits, axis=0, keepdims=True)
        raised = jnp.exp(logits - top)
        weights = raised / jnp.sum(raised, axis=0, keepdims=True)
        spread = jnp.concatenate([jnp.where(user == u + 1, weights, 0.0) for u in range(lanes // caps)], axis=0)
        part = dot(spread.astype(BF16), rows_refs[s][...])
        if s == 0:
            summed_ref[...] = part
        else:
            summed_ref[...] += part


def chosen(values, user, caps):
    total = jnp.zeros((caps, user.shape[1]), F32)
    for u in range(values.shape[0] // caps):
        total = jnp.where(user == u + 1, values[u * caps : (u + 1) * caps], total)
    return total


def products(rows_refs, user_ref, summed_ref, sent_ref, caps):
    owners, room = len(rows_refs), rows_refs[0].shape[0]
    summed = summed_ref[...]
    lanes = summed.shape[0]
    high = summed.astype(BF16)
    low = (summed - high.astype(F32)).astype(BF16)
    both = jnp.concatenate([high, low], axis=0)
    for s in range(owners):
        dots = dot_nt(both, rows_refs[s][...])
        dots = dots[:lanes] + dots[lanes:]
        sent_ref[s * caps : (s + 1) * caps, :room] = chosen(dots, user_ref[s : s + 1, :], caps)
    sent_ref[:lanes, room:] = jnp.broadcast_to(
        jnp.sum(summed * summed, axis=1, keepdims=True), (lanes, sent_ref.shape[1] - room)
    )
    if sent_ref.shape[0] > lanes:
        sent_ref[lanes:, room:] = jnp.zeros((sent_ref.shape[0] - lanes, sent_ref.shape[1] - room), F32)


def first_kernel(*refs, owners):
    rows_refs, (seed_ref, user_ref, table_ref, logits_ref, sent_ref, summed_ref) = refs[:owners], refs[owners:]
    caps, seeds = table_ref.shape
    room = rows_refs[0].shape[0]

    def initial(s):
        onehot = jnp.where(iota((seeds, room), 0) == seed_ref[s : s + 1, :], 1.0, 0.0)
        return jnp.dot(table_ref[...], onehot, precision=lax.Precision.HIGHEST, preferred_element_type=F32)

    route(initial, rows_refs, user_ref, summed_ref, logits_ref)
    products(rows_refs, user_ref, summed_ref, sent_ref, caps)


def later_kernel(*refs, cols, last, owners, lanes):
    parts, rows_refs, refs = refs[:cols], refs[cols : cols + owners], refs[cols + owners :]
    (user_ref, old_ref), outs = refs[:2], refs[2:]
    room = rows_refs[0].shape[0]
    caps = old_ref.shape[1]
    squares = sum(part[:lanes, room : room + 1] for part in parts)
    scale = squash_scale(squares)

    def updated(s):
        dots = sum(part[s * caps : (s + 1) * caps, :room] for part in parts)
        user = user_ref[s : s + 1, :]
        wide = jnp.broadcast_to(scale, (lanes, room))
        return old_ref[s] + dots * chosen(wide, user, caps)

    if last:
        summed_ref, square_ref = outs
        route(updated, rows_refs, user_ref, summed_ref, None)
        summed = summed_ref[...]
        square_ref[...] = jnp.broadcast_to(jnp.sum(summed * summed, axis=1, keepdims=True), square_ref.shape)
    else:
        logits_ref, sent_ref, summed_ref = outs
        route(updated, rows_refs, user_ref, summed_ref, logits_ref)
        products(rows_refs, user_ref, summed_ref, sent_ref, caps)


def squash_kernel(summed_ref, *refs):
    scale = squash_scale(sum(part[:, :1] for part in refs[:-1]))
    refs[-1][...] = summed_ref[...] * scale


def call(kernel, out_shape, n_in, smem=(), flops=0, mib=16, **kw):
    ins = [SMEM if i in smem else VMEM for i in range(n_in)]
    size = sum(math.prod(leaf.shape) * leaf.dtype.itemsize for leaf in jax.tree.leaves(out_shape))
    return pl.pallas_call(
        kernel,
        out_shape=out_shape,
        in_specs=ins,
        out_specs=jax.tree.map(lambda _: VMEM, out_shape),
        compiler_params=pltpu.CompilerParams(vmem_limit_bytes=mib << 20),
        cost_estimate=pl.CostEstimate(flops=flops, bytes_accessed=size, transcendentals=0),
        **kw,
    )


def shifted(x, by):
    cols = lax.axis_size("cols")
    return lax.ppermute(x, "cols", [((i + by) % cols, i) for i in range(cols)])


def all_cols(x):
    return [x] + [shifted(x, by) for by in range(1, lax.axis_size("cols"))]


def owner_ranks(owner, owners):
    tok_count = owner.shape[0]
    span = min(256, tok_count)
    onehot = (owner[:, None] == jnp.arange(owners, dtype=I32)[None, :]).astype(F32)
    blocked = onehot.reshape(tok_count // span, span, owners)
    lower = (iota((span, span), 0) >= iota((span, span), 1)).astype(F32)
    within = jnp.einsum("ij,bjo->bio", lower, blocked)
    totals = within[:, -1, :]
    before = jnp.cumsum(totals, axis=0) - totals
    counts = (within + before[:, None, :]).reshape(tok_count, owners)
    return (jnp.sum(counts * onehot, axis=1) - 1.0).astype(I32)


def any_input(item_ids, lengths, seed_rows, mapped_rows, seed_table, cap):
    users_here, hist = item_ids.shape
    owners = lax.axis_size("users")
    rows_dev, half = mapped_rows.shape
    tok_count = users_here * hist
    flat_ids = item_ids.reshape(tok_count)
    owner = flat_ids // rows_dev
    slot = owner * cap + owner_ranks(owner, owners)
    requests = jnp.zeros((owners * cap,), I32).at[slot].set(flat_ids % rows_dev).reshape(owners, cap)
    asked = lax.all_to_all(requests, "users", split_axis=0, concat_axis=0, tiled=True)
    answers = lax.all_to_all(mapped_rows[asked], "users", split_axis=0, concat_axis=0, tiled=True)
    mapped = answers.reshape(owners * cap, half)[slot].reshape(users_here, hist, half)
    logits = seed_table[seed_rows]
    live = (jnp.arange(hist, dtype=I32)[None, :] < lengths[:, None]).astype(F32)
    for step in range(ITERS):
        weights = (jax.nn.softmax(logits, axis=-1) * live[:, :, None]).astype(BF16)
        summed = jnp.einsum("utk,utd->ukd", weights, mapped, preferred_element_type=F32)
        squares = sum(all_cols(jnp.sum(summed * summed, axis=-1)))
        scale = squash_scale(squares)
        if step + 1 < ITERS:
            dots = jnp.einsum(
                "utd,ukd->utk", mapped, summed, preferred_element_type=F32, precision=lax.Precision.HIGHEST
            )
            logits = logits + sum(all_cols(dots)) * scale[:, None, :]
    return summed * scale[:, :, None]


def cuts_of(owners):
    far = owners // 2
    return [(far, far + 1), (far + 1, far + 4), (far + 4, owners), (0, far)]


def on_device(item_ids, lengths, seed_rows, item_table, bilinear, seed_table):
    users, hist = item_ids.shape
    owners = lax.axis_size("users")
    cols = lax.axis_size("cols")
    me = lax.axis_index("users")
    rows_dev = item_table.shape[0]
    half = bilinear.shape[1]
    seeds, caps = seed_table.shape
    tok_count = users * hist
    cap = max(2, (2 * tok_count + owners - 1) // owners)
    room = -(-cap * 15 // 32 // 16) * 16
    pairs = owners * users
    lanes = users * caps
    assert owners % users == 0 and owners & (owners - 1) == 0
    assert hist <= 256 and seeds <= 256 and rows_dev * users <= 65536
    local = lax.rem(me, users)
    group = me - local
    here = me.reshape(1)

    table_parts = all_cols(item_table)
    blocks, dest = call(
        functools.partial(prep_kernel, owners=owners, rows_dev=rows_dev, seeds=seeds, cap=cap),
        (jax.ShapeDtypeStruct((owners, 1, cap + pairs + hist), I32), jax.ShapeDtypeStruct((users, 1), I32)),
        4,
        smem=(0,),
    )(local.reshape(1), item_ids, seed_rows, lengths.reshape(1, users))
    recv = lax.all_to_all(blocks, "users", split_axis=0, concat_axis=0, tiled=True)
    mapped_rows = call(
        functools.partial(map_kernel, cols=cols),
        jax.ShapeDtypeStruct((rows_dev, half), BF16),
        2 + cols,
        smem=(0,),
        flops=2 * rows_dev * half * bilinear.shape[0],
    )(lax.axis_index("cols").reshape(1), bilinear, *table_parts)
    counts = recv[:, 0, cap : cap + pairs].reshape(owners // users, users, pairs)
    fits = jnp.max(jnp.sum(counts, axis=1)) <= room

    block = jax.ShapeDtypeStruct((room, half), BF16)
    scratch = [pltpu.VMEM((room, half), BF16)]
    each = 2 * room * half * rows_dev
    rows = [None] * owners
    cuts = cuts_of(owners)
    index = order = None
    for first, stop in cuts:
        many = stop - first
        if index is None:
            index, *sends = call(
                functools.partial(index_kernel, first=first, cap=cap),
                [jax.ShapeDtypeStruct((owners // users, room, users), F32)] + [block] * many,
                3,
                smem=(0,),
                flops=many * each,
                scratch_shapes=scratch,
            )(here, recv, mapped_rows)
            order = index
        else:
            order, *sends = call(
                functools.partial(gather_kernel, first=first),
                [jax.ShapeDtypeStruct((8, 128), F32)] + [block] * many,
                4,
                smem=(0,),
                flops=many * each,
                scratch_shapes=scratch,
            )(here, index, mapped_rows, order)
        for mask, out in zip(range(first, stop), sends):
            rows[mask] = out if mask == 0 else lax.ppermute(out, "users", [(i, i ^ mask) for i in range(owners)])

    where = jax.ShapeDtypeStruct((owners, room), I32)
    seed, user = call(
        functools.partial(meta_kernel, users=users, hist=hist, rows_dev=rows_dev, seeds=seeds), (where, where), 2, smem=(0,)
    )(here, recv)
    logits_shape = jax.ShapeDtypeStruct((owners, caps, room), F32)
    wide = (room // 128 + 1) * 128
    sent_shape = jax.ShapeDtypeStruct((owners * caps, wide), F32)
    summed_shape = jax.ShapeDtypeStruct((lanes, half), F32)
    square_shape = jax.ShapeDtypeStruct((lanes, 128), F32)
    step_shapes = (logits_shape, sent_shape, summed_shape)
    kernel = functools.partial(first_kernel, owners=owners)
    logits, sent, _ = call(kernel, step_shapes, owners + 3)(*rows, seed, user, seed_table.T)
    later = functools.partial(later_kernel, cols=cols, owners=owners, lanes=lanes)
    for _ in range(ITERS - 2):
        kernel = functools.partial(later, last=False)
        logits, sent, _ = call(kernel, step_shapes, cols + owners + 2)(*all_cols(sent), *rows, user, logits)
    kernel = functools.partial(later, last=True)
    summed, square = call(kernel, (summed_shape, square_shape), cols + owners + 2)(*all_cols(sent), *rows, user, logits)
    capsules = call(squash_kernel, summed_shape, cols + 1)(summed, *all_cols(square)).reshape(users, caps, half)
    if owners > users:
        spread = jnp.zeros((owners, caps, half), F32)
        capsules = lax.dynamic_update_slice_in_dim(spread, capsules, group, 0)
    back = lax.all_to_all(capsules, "users", split_axis=0, concat_axis=0, tiled=True)
    if owners > users:
        back = lax.dynamic_slice_in_dim(back, group, users, 0)
    dealt = back[dest[:, 0]]

    def kept(dealt, *_):
        return dealt

    def full(dealt, mapped_rows, seed_table, item_ids, lengths, seed_rows):
        return any_input(item_ids, lengths, seed_rows, mapped_rows, seed_table, cap)

    return lax.cond(fits, kept, full, dealt, mapped_rows, seed_table, item_ids, lengths, seed_rows)


def solution(mesh):
    placed = (
        P("users", None),
        P("users"),
        P("users", None),
        P("users", "cols"),
        P(None, "cols"),
        P(),
    )

    return jax.shard_map(on_device, mesh=mesh, in_specs=placed, out_specs=P("users", None, "cols"), check_vma=False)
```

time: 177 us -> 174 us (0.983)
  starting transfers between devices: 30.7 us -> 82.2 us
  waiting for transfers between devices: 83.8 us -> 50.4 us
  matrix products: 9.69 us -> 0 us
  local copies, waits for them, and re-layouts: 10.1 us -> 4.18 us
  other arithmetic: 3.36 us -> 0.69 us
  Pallas kernels: 37.4 us -> 34.9 us
    ppermute x0 -> x15, starting transfers between devices: none -> 68.7 us  [on_device(): lax.ppermute(out, 'users', [(i, i ^ mask) for i in range(owners)])]
    all_to_all x2 -> x1, waiting for transfers between devices: 76.8 us -> 8.89 us  [on_device(): lax.all_to_all(capsules, 'users', split_axis=0, concat_axis=0, tiled=True)]
    ppermute x0 -> x15, waiting for transfers between devices: none -> 37.9 us  [on_device(): lax.ppermute(out, 'users', [(i, i ^ mask) for i in range(owners)])]
    all_to_all x2 -> x1, starting transfers between devices: 22 us -> 4.76 us  [on_device(): lax.all_to_all(capsules, 'users', split_axis=0, concat_axis=0, tiled=True)]
    dot_general x2 -> x0, matrix products: 9.69 us -> none  [dot(): return jnp.dot(a, b, preferred_element_type=F32)]
    another operation x2 -> x1, local copies, waits for them, and re-layouts: 4.02 us -> 0.08 us
    unnamed x13 -> x16, local copies, waits for them, and re-layouts: 0.74 us -> 3.53 us
    all_to_all x1, waiting for transfers between devices: 2.68 us -> 0.01 us  [on_device(): lax.all_to_all(blocks, 'users', split_axis=0, concat_axis=0, tiled=True)]
  transfers between devices with their start and end apart: 7 -> 21, of which waited for: 6 -> 12; matrix products, arithmetic and copies ran while one was open for 5% -> 0% of each run, Pallas kernels for 4% -> 5%
where the time goes in v2:
time: 174 us; the launch traced here: 173 us
  starting transfers between devices  82.2 us (47%)
  waiting for transfers between devices  50.4 us (29%)
  Pallas kernels  34.9 us (20%)
  local copies, waits for them, and re-layouts  4.18 us (2%)
    ppermute x15, starting transfers between devices, on_device(): lax.ppermute(out, 'users', [(i, i ^ mask) for i in range(owners)])  68.7 us
    ppermute x15, waiting for transfers between devices, on_device(): lax.ppermute(out, 'users', [(i, i ^ mask) for i in range(owners)])  37.9 us
    pallas_call x3, Pallas kernels, on_device(): call(functools.partial(gather_kernel, first=first), [jax.ShapeDtypeStruct...  13.6 us
    all_to_all x1, waiting for transfers between devices, on_device(): lax.all_to_all(capsules, 'users', split_axis=0, concat_axis=0, tiled=True)  8.89 us
    all_to_all x1, starting transfers between devices, on_device(): lax.all_to_all(blocks, 'users', split_axis=0, concat_axis=0, tiled=True)  7.85 us
    pallas_call x1, Pallas kernels, on_device(): call(functools.partial(index_kernel, first=first, cap=cap), [jax.ShapeDty...  5.06 us
    pallas_call x1, Pallas kernels, on_device(): call(functools.partial(map_kernel, cols=cols), jax.ShapeDtypeStruct((rows...  4.83 us
    all_to_all x1, starting transfers between devices, on_device(): lax.all_to_all(capsules, 'users', split_axis=0, concat_axis=0, tiled=True)  4.76 us
  transfers between devices with their start and end apart: 21, of which 12 were waited for; matrix products, arithmetic and copies ran while one was open for 0% of the time, Pallas kernels for 5%

profile of v2, /device:TPU:0, one launch (start us, length us, event | category | flops | bytes accessed | tf_op | source)
XLA Modules:
  0.0 173.4 jit_solution(9055441925525916071)
XLA Ops:
  0.5 3.4 %shard_map.66 = (s32[16,1,1024]{2,1,0:T(1,128)}, s32[16,1]{1,0:T(8,128)S(1)}) custom-call(s32[1]{0:T(128)} %bitcast.11.local_ref, s32[16,256]{1,0:T(8,128)} %ids_ref.1, s32[16,256]{1,0:T(8,128)} %seeds_ref.1, s32[1,16]{1,0:T(1,128)} %bitcast.68), custom_call_target="tpu_custom_call" | custom-call | bytes 65600 | tf_op jit(solution)/shard_map/pallas_call | solution.py:381
  3.9 7.9 %all-to-all-start.2 = ((s32[16,1,1024]{2,1,0:T(1,128)}), s32[16,1,1024]{2,1,0:T(1,128)S(1)}, u32[]{:S(2)}, u32[]{:S(2)}) async-start(s32[16,1,1024]{2,1,0:T(1,128)} %get-tuple-element.69), calls=%async_computation.2 | async-start | bytes 131072 | tf_op jit(solution)/shard_map/all_to_all | solution.py:387
  11.7 1.6 copy-done
  14.5 4.8 %shard_map.67.mapped_ref = bf16[2048,512]{1,0:T(8,128)(2,1)} custom-call(s32[1]{0:T(128)} %bitcast.13.refs_0_, bf16[1024,512]{1,0:T(8,128)(2,1)S(1)} %copy-done.1, bf16[2048,512]{1,0:T(8,128)(2,1)S(1)} %copy-done, bf16[2048,512]{1,0:T(8,128)(2,1)S(1)} %collective-permute-done.5.refs_3_), custom_call_target="tpu_custom_call" | custom-call | flops 2147483648 | bytes 2097152 | tf_op jit(solution)/shard_map/pallas_call | solution.py:388
  19.4 5.1 %shard_map.68 = (f32[1,240,16]{2,1,0:T(8,128)S(1)}, bf16[240,512]{1,0:T(8,128)(2,1)S(1)}) custom-call(s32[1]{0:T(128)} %bitcast.14.me_ref, s32[16,1,1024]{2,1,0:T(1,128)S(1)} %all-to-all-done.2.recv_ref, bf16[2048,512]{1,0:T(8,128)(2,1)} %shard_map.67.mapped_ref), custom_call_target="tpu_custom_call" | custom-call | flops 503316480 | bytes 261120 | tf_op jit(solution)/shard_map/pallas_call | solution.py:407
  24.5 3.8 %shard_map.69 = (f32[8,128]{1,0:T(8,128)S(1)}, bf16[240,512]{1,0:T(8,128)(2,1)S(1)}, bf16[240,512]{1,0:T(8,128)(2,1)S(1)}, bf16[240,512]{1,0:T(8,128)(2,1)S(1)}) custom-call(s32[1]{0:T(128)} %bitcast.14.me_ref, f32[1,240,16]{2,1,0:T(8,128)S(1)} %get-tuple-element.71.index_ref.after_ref, bf16[2048,512]{1,0:T(8,128)(2,1)} %shard_map.67.mapped_ref, ...), custom_call_target="tpu_custom_call" | custom-call | flops 1509949440 | bytes 741376 | tf_op jit(solution)/shard_map/pallas_call | solution.py:417
  28.3 3.0 %shard_map.70 = (f32[8,128]{1,0:T(8,128)S(1)}, bf16[240,512]{1,0:T(8,128)(2,1)S(1)}, bf16[240,512]{1,0:T(8,128)(2,1)S(1)}, bf16[240,512]{1,0:T(8,128)(2,1)S(1)}, bf16[240,512]{1,0:T(8,128)(2,1)S(1)}) custom-call(s32[1]{0:T(128)} %bitcast.14.me_ref, f32[1,240,16]{2,1,0:T(8,128)S(1)} %get-tuple-element.71.index_ref.after_ref, bf16[2048,512]{1,0:T(8,128)(2,1)S(1)} %copy-done.2, ...), custom_call_target="tpu_custom_call" | custom-call | flops 2013265920 | bytes 987136 | tf_op jit(solution)/shard_map/pallas_call | solution.py:417
  31.3 6.7 %shard_map.71 = (f32[8,128]{1,0:T(8,128)}, bf16[240,512]{1,0:T(8,128)(2,1)S(1)}, bf16[240,512]{1,0:T(8,128)(2,1)S(1)}, bf16[240,512]{1,0:T(8,128)(2,1)S(1)}, bf1...) custom-call(s32[1]{0:T(128)} %bitcast.14.me_ref, ...), custom_call_target="tpu_custom_call" | custom-call | flops 4026531840 | bytes 1970176 | tf_op jit(solution)/shard_map/pallas_call | solution.py:417
  38.1 2.8 %collective-permute-start.10 = (bf16[240,512]{1,0:T(8,128)(2,1)S(1)}, bf16[240,512]{1,0:T(8,128)(2,1)S(1)}, u32[]{:S(2)}, u32[]{:S(2)}) collective-permute-start(bf16[240,512]{1,0:T(8,128)(2,1)S(1)} %get-tuple-element.79), channel_id=1, source_target_pairs={{0,10},{2,8},{4,14},{6,12},{8,2},{10,0},{12,6},{14,4},{16,26},{18,... | collective-permute-start | bytes 737288 | tf_op jit(solution)/shard_map/ppermute | solution.py:426
  40.9 1.5 collective-permute-start.11
  42.3 1.5 collective-permute-start.12
  43.8 1.5 collective-permute-start.6
  45.3 1.5 collective-permute-start.7
  47.8 2.8 %collective-permute-start.8 = (bf16[240,512]{1,0:T(8,128)(2,1)S(1)}, bf16[240,512]{1,0:T(8,128)(2,1)S(1)}, u32[]{:S(2)}, u32[]{:S(2)}) collective-permute-start(bf16[240,512]{1,0:T(8,128)(2,1)S(1)} %get-tuple-element.77), channel_id=1, source_target_pairs={{0,6},{2,4},{4,2},{6,0},{8,14},{10,12},{12,10},{14,8},{16,22},{18,... | collective-permute-start | bytes 737288 | tf_op jit(solution)/shard_map/ppermute | solution.py:426
  50.6 4.2 %collective-permute-done.11.refs_6_.refs_8_ = bf16[240,512]{1,0:T(8,128)(2,1)S(1)} collective-permute-done((bf16[240,512]{1,0:T(8,128)(2,1)S(1)}, bf16[240,512]{1,0:T(8,128)(2,1)S(1)}, u32[]{:S(2)}, u32[]{:S(2)}) %collective-permute-start.11) | collective-permute-done | bytes 245792 | tf_op jit(solution)/shard_map/ppermute | solution.py:426
  56.1 3.9 %collective-permute-done.12.refs_7_.refs_9_ = bf16[240,512]{1,0:T(8,128)(2,1)S(1)} collective-permute-done((bf16[240,512]{1,0:T(8,128)(2,1)S(1)}, bf16[240,512]{1,0:T(8,128)(2,1)S(1)}, u32[]{:S(2)}, u32[]{:S(2)}) %collective-permute-start.12) | collective-permute-done | bytes 245792 | tf_op jit(solution)/shard_map/ppermute | solution.py:426
  60.0 3.1 %collective-permute-start.17 = (bf16[240,512]{1,0:T(8,128)(2,1)S(1)}, bf16[240,512]{1,0:T(8,128)(2,1)S(1)}, u32[]{:S(2)}, u32[]{:S(2)}) collective-permute-start(bf16[240,512]{1,0:T(8,128)(2,1)S(1)} %get-tuple-element.86), channel_id=1, source_target_pairs={{0,24},{2,26},{4,28},{6,30},{8,16},{10,18},{12,20},{14,22},{16,8},... | collective-permute-start | bytes 737288 | tf_op jit(solution)/shard_map/ppermute | solution.py:426
  64.5 3.3 %collective-permute-done.7.refs_2_.refs_4_ = bf16[240,512]{1,0:T(8,128)(2,1)S(1)} collective-permute-done((bf16[240,512]{1,0:T(8,128)(2,1)S(1)}, bf16[240,512]{1,0:T(8,128)(2,1)S(1)}, u32[]{:S(2)}, u32[]{:S(2)}) %collective-permute-start.7) | collective-permute-done | bytes 245792 | tf_op jit(solution)/shard_map/ppermute | solution.py:426
  67.8 3.3 %collective-permute-start.19 = (bf16[240,512]{1,0:T(8,128)(2,1)S(1)}, bf16[240,512]{1,0:T(8,128)(2,1)S(1)}, u32[]{:S(2)}, u32[]{:S(2)}) collective-permute-start(bf16[240,512]{1,0:T(8,128)(2,1)S(1)} %get-tuple-element.88), channel_id=1, source_target_pairs={{0,28},{2,30},{4,24},{6,26},{8,20},{10,22},{12,16},{14,18},{16,12}... | collective-permute-start | bytes 737288 | tf_op jit(solution)/shard_map/ppermute | solution.py:426
  71.0 1.5 collective-permute-start.20
  72.5 1.5 collective-permute-start.14
  74.0 23.3 %collective-permute-start.15 = (bf16[240,512]{1,0:T(8,128)(2,1)S(1)}, bf16[240,512]{1,0:T(8,128)(2,1)S(1)}, u32[]{:S(2)}, u32[]{:S(2)}) collective-permute-start(bf16[240,512]{1,0:T(8,128)(2,1)S(1)} %get-tuple-element.84), channel_id=1, source_target_pairs={{0,20},{2,22},{4,16},{6,18},{8,28},{10,30},{12,24},{14,26},{16,4},... | collective-permute-start | bytes 737288 | tf_op jit(solution)/shard_map/ppermute | solution.py:426
  97.3 14.1 %collective-permute-start.16 = (bf16[240,512]{1,0:T(8,128)(2,1)S(1)}, bf16[240,512]{1,0:T(8,128)(2,1)S(1)}, u32[]{:S(2)}, u32[]{:S(2)}) collective-permute-start(bf16[240,512]{1,0:T(8,128)(2,1)S(1)} %get-tuple-element.85), channel_id=1, source_target_pairs={{0,22},{2,20},{4,18},{6,16},{8,30},{10,28},{12,26},{14,24},{16,6},... | collective-permute-start | bytes 737288 | tf_op jit(solution)/shard_map/ppermute | solution.py:426
  111.3 7.9 %collective-permute-start.13 = (bf16[240,512]{1,0:T(8,128)(2,1)S(1)}, bf16[240,512]{1,0:T(8,128)(2,1)S(1)}, u32[]{:S(2)}, u32[]{:S(2)}) collective-permute-start(bf16[240,512]{1,0:T(8,128)(2,1)S(1)} %get-tuple-element.82), channel_id=1, source_target_pairs={{0,16},{2,18},{4,20},{6,22},{8,24},{10,26},{12,28},{14,30},{16,0},... | collective-permute-start | bytes 737288 | tf_op jit(solution)/shard_map/ppermute | solution.py:426
  120.6 12.6 %collective-permute-done.14.refs_9_.refs_11_ = bf16[240,512]{1,0:T(8,128)(2,1)S(1)} collective-permute-done((bf16[240,512]{1,0:T(8,128)(2,1)S(1)}, bf16[240,512]{1,0:T(8,128)(2,1)S(1)}, u32[]{:S(2)}, u32[]{:S(2)}) %collective-permute-start.14) | collective-permute-done | bytes 245792 | tf_op jit(solution)/shard_map/ppermute | solution.py:426
  133.1 5.0 %collective-permute-done.15.refs_10_.refs_12_ = bf16[240,512]{1,0:T(8,128)(2,1)S(1)} collective-permute-done((bf16[240,512]{1,0:T(8,128)(2,1)S(1)}, bf16[240,512]{1,0:T(8,128)(2,1)S(1)}, u32[]{:S(2)}, u32[]{:S(2)}) %collective-permute-start.15) | collective-permute-done | bytes 245792 | tf_op jit(solution)/shard_map/ppermute | solution.py:426
  138.1 5.8 %collective-permute-done.16.refs_11_.refs_13_ = bf16[240,512]{1,0:T(8,128)(2,1)S(1)} collective-permute-done((bf16[240,512]{1,0:T(8,128)(2,1)S(1)}, bf16[240,512]{1,0:T(8,128)(2,1)S(1)}, u32[]{:S(2)}, u32[]{:S(2)}) %collective-permute-start.16) | collective-permute-done | bytes 245792 | tf_op jit(solution)/shard_map/ppermute | solution.py:426
  143.9 2.1 %collective-permute-done.13.refs_8_.refs_10_ = bf16[240,512]{1,0:T(8,128)(2,1)S(1)} collective-permute-done((bf16[240,512]{1,0:T(8,128)(2,1)S(1)}, bf16[240,512]{1,0:T(8,128)(2,1)S(1)}, u32[]{:S(2)}, u32[]{:S(2)}) %collective-permute-start.13) | collective-permute-done | bytes 245792 | tf_op jit(solution)/shard_map/ppermute | solution.py:426
  145.9 2.8 %shard_map.73 = (f32[16,8,240]{2,1,0:T(8,128)S(1)}, f32[128,256]{1,0:T(8,128)S(1)}, f32[128,512]{1,0:T(8,128)}) custom-call(bf16[240,512]{1,0:T(8,128)(2,1)S(1)} %get-tuple-element.74.refs_0_.refs_2_, bf16[240,512]{1,0:T(8,128)(2,1)S(1)} %collective-permute-done.6.refs_1_.refs_3_, bf16[240,512]{1,0:T(8,128)(2,1)S(1)} %collective-permute-done.7.refs_2_.refs_4_, ...), custom_call_target="tpu_custom_call" | custom-call | bytes 516096 | tf_op jit(solution)/shard_map/pallas_call | solution.py:439
  150.1 2.2 %shard_map.74 = (f32[16,8,240]{2,1,0:T(8,128)S(1)}, f32[128,256]{1,0:T(8,128)S(1)}, f32[128,512]{1,0:T(8,128)}) custom-call(f32[128,256]{1,0:T(8,128)S(1)} %get-tuple-element.92.refs_0_, f32[128,256]{1,0:T(8,128)S(1)} %collective-permute-done.21.refs_1_, bf16[240,512]{1,0:T(8,128)(2,1)S(1)} %get-tuple-element.74.refs_0_.refs_2_, ...), custom_call_target="tpu_custom_call" | custom-call | bytes 516096 | tf_op jit(solution)/shard_map/pallas_call | solution.py:443
  156.8 4.8 %all-to-all-start.3 = ((f32[16,8,512]{2,1,0:T(8,128)}), f32[16,8,512]{2,1,0:T(8,128)S(1)}, u32[]{:S(2)}, u32[]{:S(2)}) async-start(f32[16,8,512]{2,1,0:T(8,128)} %bitcast.16), calls=%async_computation.3 | async-start | bytes 524288 | tf_op jit(solution)/shard_map/all_to_all | solution.py:450
  162.9 8.9 %all-to-all-done.3 = f32[16,8,512]{2,1,0:T(8,128)S(1)} async-done(((f32[16,8,512]{2,1,0:T(8,128)}), f32[16,8,512]{2,1,0:T(8,128)S(1)}, u32[]{:S(2)}, u32[]{:S(2)}) %all-to-all-start.3) | async-done | bytes 262176 | tf_op jit(solution)/shard_map/all_to_all | solution.py:450
  (44 shorter events, 15.5 us)
Async XLA Ops:
  0.0 11.7 %collective-permute-start.5 = (bf16[2048,512]{1,0:T(8,128)(2,1)}, bf16[2048,512]{1,0:T(8,128)(2,1)S(1)}, u32[]{:S(2)}, u32[]{:S(2)}) collective-permute-start(bf16[2048,512]{1,0:T(8,128)(2,1)} %refs_2_.1), channel_id=1, source_target_pairs={{1,0},{0,1},{3,2},{2,3},{5,4},{4,5},{7,6},{6,7},{9,8},{8,9},{11,10... | collective-permute-start | bytes 6291464 | tf_op jit(solution)/shard_map/ppermute | solution.py:309
  3.9 15.5 %all-to-all-start.2 = ((s32[16,1,1024]{2,1,0:T(1,128)}), s32[16,1,1024]{2,1,0:T(1,128)S(1)}, u32[]{:S(2)}, u32[]{:S(2)}) async-start(s32[16,1,1024]{2,1,0:T(1,128)} %get-tuple-element.69), calls=%async_computation.2 | async-start | bytes 131072 | tf_op jit(solution)/shard_map/all_to_all | solution.py:387
  11.7 1.6 copy-start
  13.3 1.2 copy-start.1
  19.4 8.9 %copy-start.2 = (bf16[2048,512]{1,0:T(8,128)(2,1)S(1)}, bf16[2048,512]{1,0:T(8,128)(2,1)}, u32[]{:S(2)}) copy-start(bf16[2048,512]{1,0:T(8,128)(2,1)} %shard_map.67.mapped_ref) | copy-start | bytes 6291460
  31.3 114.6 %copy-start.7 = (f32[64,8]{0,1:T(8,128)S(1)}, f32[64,8]{0,1:T(8,128)}, u32[]{:S(2)}) copy-start(f32[64,8]{0,1:T(8,128)} %param.13) | copy-start | bytes 6148
  38.1 9.7 %collective-permute-start.10 = (bf16[240,512]{1,0:T(8,128)(2,1)S(1)}, bf16[240,512]{1,0:T(8,128)(2,1)S(1)}, u32[]{:S(2)}, u32[]{:S(2)}) collective-permute-start(bf16[240,512]{1,0:T(8,128)(2,1)S(1)} %get-tuple-element.79), channel_id=1, source_target_pairs={{0,10},{2,8},{4,14},{6,12},{8,2},{10,0},{12,6},{14,4},{16,26},{18,... | collective-permute-start | bytes 737288 | tf_op jit(solution)/shard_map/ppermute | solution.py:426
  40.9 13.9 %collective-permute-start.11 = (bf16[240,512]{1,0:T(8,128)(2,1)S(1)}, bf16[240,512]{1,0:T(8,128)(2,1)S(1)}, u32[]{:S(2)}, u32[]{:S(2)}) collective-permute-start(bf16[240,512]{1,0:T(8,128)(2,1)S(1)} %get-tuple-element.80), channel_id=1, source_target_pairs={{0,12},{2,14},{4,8},{6,10},{8,4},{10,6},{12,0},{14,2},{16,28},{18,... | collective-permute-start | bytes 737288 | tf_op jit(solution)/shard_map/ppermute | solution.py:426
  42.3 17.7 %collective-permute-start.12 = (bf16[240,512]{1,0:T(8,128)(2,1)S(1)}, bf16[240,512]{1,0:T(8,128)(2,1)S(1)}, u32[]{:S(2)}, u32[]{:S(2)}) collective-permute-start(bf16[240,512]{1,0:T(8,128)(2,1)S(1)} %get-tuple-element.81), channel_id=1, source_target_pairs={{0,14},{2,12},{4,10},{6,8},{8,6},{10,4},{12,2},{14,0},{16,30},{18,... | collective-permute-start | bytes 737288 | tf_op jit(solution)/shard_map/ppermute | solution.py:426
  43.8 19.4 %collective-permute-start.6 = (bf16[240,512]{1,0:T(8,128)(2,1)S(1)}, bf16[240,512]{1,0:T(8,128)(2,1)S(1)}, u32[]{:S(2)}, u32[]{:S(2)}) collective-permute-start(bf16[240,512]{1,0:T(8,128)(2,1)S(1)} %get-tuple-element.75), channel_id=1, source_target_pairs={{0,2},{2,0},{4,6},{6,4},{8,10},{10,8},{12,14},{14,12},{16,18},{18,... | collective-permute-start | bytes 737288 | tf_op jit(solution)/shard_map/ppermute | solution.py:426
  45.3 22.5 %collective-permute-start.7 = (bf16[240,512]{1,0:T(8,128)(2,1)S(1)}, bf16[240,512]{1,0:T(8,128)(2,1)S(1)}, u32[]{:S(2)}, u32[]{:S(2)}) collective-permute-start(bf16[240,512]{1,0:T(8,128)(2,1)S(1)} %get-tuple-element.76), channel_id=1, source_target_pairs={{0,4},{2,6},{4,0},{6,2},{8,12},{10,14},{12,8},{14,10},{16,20},{18,... | collective-permute-start | bytes 737288 | tf_op jit(solution)/shard_map/ppermute | solution.py:426
  47.8 23.2 %collective-permute-start.8 = (bf16[240,512]{1,0:T(8,128)(2,1)S(1)}, bf16[240,512]{1,0:T(8,128)(2,1)S(1)}, u32[]{:S(2)}, u32[]{:S(2)}) collective-permute-start(bf16[240,512]{1,0:T(8,128)(2,1)S(1)} %get-tuple-element.77), channel_id=1, source_target_pairs={{0,6},{2,4},{4,2},{6,0},{8,14},{10,12},{12,10},{14,8},{16,22},{18,... | collective-permute-start | bytes 737288 | tf_op jit(solution)/shard_map/ppermute | solution.py:426
  54.8 17.7 %collective-permute-start.9 = (bf16[240,512]{1,0:T(8,128)(2,1)S(1)}, bf16[240,512]{1,0:T(8,128)(2,1)S(1)}, u32[]{:S(2)}, u32[]{:S(2)}) collective-permute-start(bf16[240,512]{1,0:T(8,128)(2,1)S(1)} %get-tuple-element.78), channel_id=1, source_target_pairs={{0,8},{2,10},{4,12},{6,14},{8,0},{10,2},{12,4},{14,6},{16,24},{18,... | collective-permute-start | bytes 737288 | tf_op jit(solution)/shard_map/ppermute | solution.py:426
  60.0 13.9 %collective-permute-start.17 = (bf16[240,512]{1,0:T(8,128)(2,1)S(1)}, bf16[240,512]{1,0:T(8,128)(2,1)S(1)}, u32[]{:S(2)}, u32[]{:S(2)}) collective-permute-start(bf16[240,512]{1,0:T(8,128)(2,1)S(1)} %get-tuple-element.86), channel_id=1, source_target_pairs={{0,24},{2,26},{4,28},{6,30},{8,16},{10,18},{12,20},{14,22},{16,8},... | collective-permute-start | bytes 737288 | tf_op jit(solution)/shard_map/ppermute | solution.py:426
  63.2 34.1 %collective-permute-start.18 = (bf16[240,512]{1,0:T(8,128)(2,1)S(1)}, bf16[240,512]{1,0:T(8,128)(2,1)S(1)}, u32[]{:S(2)}, u32[]{:S(2)}) collective-permute-start(bf16[240,512]{1,0:T(8,128)(2,1)S(1)} %get-tuple-element.87), channel_id=1, source_target_pairs={{0,26},{2,24},{4,30},{6,28},{8,18},{10,16},{12,22},{14,20},{16,10}... | collective-permute-start | bytes 737288 | tf_op jit(solution)/shard_map/ppermute | solution.py:426
  67.8 43.6 %collective-permute-start.19 = (bf16[240,512]{1,0:T(8,128)(2,1)S(1)}, bf16[240,512]{1,0:T(8,128)(2,1)S(1)}, u32[]{:S(2)}, u32[]{:S(2)}) collective-permute-start(bf16[240,512]{1,0:T(8,128)(2,1)S(1)} %get-tuple-element.88), channel_id=1, source_target_pairs={{0,28},{2,30},{4,24},{6,26},{8,20},{10,22},{12,16},{14,18},{16,12}... | collective-permute-start | bytes 737288 | tf_op jit(solution)/shard_map/ppermute | solution.py:426
  71.0 49.5 %collective-permute-start.20 = (bf16[240,512]{1,0:T(8,128)(2,1)S(1)}, bf16[240,512]{1,0:T(8,128)(2,1)S(1)}, u32[]{:S(2)}, u32[]{:S(2)}) collective-permute-start(bf16[240,512]{1,0:T(8,128)(2,1)S(1)} %get-tuple-element.89), channel_id=1, source_target_pairs={{0,30},{2,28},{4,26},{6,24},{8,22},{10,20},{12,18},{14,16},{16,14}... | collective-permute-start | bytes 737288 | tf_op jit(solution)/shard_map/ppermute | solution.py:426
  72.5 60.6 %collective-permute-start.14 = (bf16[240,512]{1,0:T(8,128)(2,1)S(1)}, bf16[240,512]{1,0:T(8,128)(2,1)S(1)}, u32[]{:S(2)}, u32[]{:S(2)}) collective-permute-start(bf16[240,512]{1,0:T(8,128)(2,1)S(1)} %get-tuple-element.83), channel_id=1, source_target_pairs={{0,18},{2,16},{4,22},{6,20},{8,26},{10,24},{12,30},{14,28},{16,2},... | collective-permute-start | bytes 737288 | tf_op jit(solution)/shard_map/ppermute | solution.py:426
  74.0 64.2 %collective-permute-start.15 = (bf16[240,512]{1,0:T(8,128)(2,1)S(1)}, bf16[240,512]{1,0:T(8,128)(2,1)S(1)}, u32[]{:S(2)}, u32[]{:S(2)}) collective-permute-start(bf16[240,512]{1,0:T(8,128)(2,1)S(1)} %get-tuple-element.84), channel_id=1, source_target_pairs={{0,20},{2,22},{4,16},{6,18},{8,28},{10,30},{12,24},{14,26},{16,4},... | collective-permute-start | bytes 737288 | tf_op jit(solution)/shard_map/ppermute | solution.py:426
  97.3 46.6 %collective-permute-start.16 = (bf16[240,512]{1,0:T(8,128)(2,1)S(1)}, bf16[240,512]{1,0:T(8,128)(2,1)S(1)}, u32[]{:S(2)}, u32[]{:S(2)}) collective-permute-start(bf16[240,512]{1,0:T(8,128)(2,1)S(1)} %get-tuple-element.85), channel_id=1, source_target_pairs={{0,22},{2,20},{4,18},{6,16},{8,30},{10,28},{12,26},{14,24},{16,6},... | collective-permute-start | bytes 737288 | tf_op jit(solution)/shard_map/ppermute | solution.py:426
  111.3 34.6 %collective-permute-start.13 = (bf16[240,512]{1,0:T(8,128)(2,1)S(1)}, bf16[240,512]{1,0:T(8,128)(2,1)S(1)}, u32[]{:S(2)}, u32[]{:S(2)}) collective-permute-start(bf16[240,512]{1,0:T(8,128)(2,1)S(1)} %get-tuple-element.82), channel_id=1, source_target_pairs={{0,16},{2,18},{4,20},{6,22},{8,24},{10,26},{12,28},{14,30},{16,0},... | collective-permute-start | bytes 737288 | tf_op jit(solution)/shard_map/ppermute | solution.py:426
  148.7 1.3 collective-permute-start.21
  150.1 21.7 %copy-start.5 = (s32[16,256]{1,0:T(8,128)S(1)}, s32[16,256]{1,0:T(8,128)}, u32[]{:S(2)}) copy-start(s32[16,256]{1,0:T(8,128)} %ids_ref.1) | copy-start | bytes 49156
  150.1 21.7 %copy-start.6 = (s32[16,256]{1,0:T(8,128)S(1)}, s32[16,256]{1,0:T(8,128)}, u32[]{:S(2)}) copy-start(s32[16,256]{1,0:T(8,128)} %seeds_ref.1) | copy-start | bytes 49156
  150.1 21.7 %copy-start.8 = (s32[16]{0:T(128)S(1)}, s32[16]{0:T(128)}, u32[]{:S(2)}) copy-start(s32[16]{0:T(128)} %param.9) | copy-start | bytes 196
  152.3 1.4 collective-permute-start.22
  154.7 1.3 collective-permute-start.23
  156.8 15.0 %all-to-all-start.3 = ((f32[16,8,512]{2,1,0:T(8,128)}), f32[16,8,512]{2,1,0:T(8,128)S(1)}, u32[]{:S(2)}, u32[]{:S(2)}) async-start(f32[16,8,512]{2,1,0:T(8,128)} %bitcast.16), calls=%async_computation.3 | async-start | bytes 524288 | tf_op jit(solution)/shard_map/all_to_all | solution.py:450
  172.7 0.7 copy-start.4

commit v3 on v2

--- a/solution.py
+++ b/solution.py
@@ -10,10 +10,13 @@
 
 
 ITERS = 3
+PLANE = 4
+RELAYS = ((1, 2), (2, 4), (0, 1))
 F32, BF16, I32 = jnp.float32, jnp.bfloat16, jnp.int32
 NT = (((1,), (1,)), ((), ()))
 VMEM = pl.BlockSpec(memory_space=pltpu.VMEM)
 SMEM = pl.BlockSpec(memory_space=pltpu.SMEM)
+FAR = pl.BlockSpec(memory_space=pltpu.HBM)
 
 
 def squash_scale(squares):
@@ -73,7 +76,9 @@
     col = jnp.sum(jnp.where(i == j, row.astype(F32), 0.0), axis=1, keepdims=True).astype(I32)
     ahead = (row > col) | ((row == col) & (i < j))
     rank = jnp.sum(jnp.where(ahead, 1.0, 0.0), axis=1, keepdims=True).astype(I32)
-    dest = div_mod(rank + local_ref[0], users)[1]
+    turn = div_mod(rank + local_ref[0], users)[1]
+    high, low = div_mod(turn, users // PLANE)
+    dest = low * PLANE + high
     dest_ref[...] = dest
     live = iota((users, hist), 1) < col
     packed = jnp.where(live, ids_ref[...] * seeds + seeds_ref[...], -1)
@@ -102,21 +107,35 @@
 
 
 def map_kernel(*refs, cols):
-    at_ref, factor_ref, parts, (out_ref,) = refs[0], refs[1], refs[2 : 2 + cols], refs[2 + cols :]
-    rows, width = parts[0].shape
-    tall = min(256, rows)
-
-    def one(i, carry):
-        here = pl.ds(pl.multiple_of(i * tall, tall), tall)
+    at_ref, factor_ref, own_ref, others = refs[0], refs[1], refs[2], refs[3 : 2 + cols]
+    out_ref, factor, own, block, done = refs[2 + cols :]
+    rows, width = own_ref.shape
+    tall = own.shape[1]
+    tiles = rows // tall
+
+    def fetch(i):
+        return pltpu.make_async_copy(own_ref.at[pl.ds(i * tall, tall)], own.at[i], done.at[i])
+
+    def store(i):
+        return pltpu.make_async_copy(block.at[i], out_ref.at[pl.ds(i * tall, tall)], done.at[tiles + i])
+
+    whole = pltpu.make_async_copy(factor_ref, factor, done.at[2 * tiles])
+    whole.start()
+    for i in range(tiles):
+        fetch(i).start()
+    whole.wait()
+    for i in range(tiles):
+        fetch(i).wait()
         total = None
-        for by, part in enumerate(parts):
+        for by in range(cols):
+            part = own[i] if by == 0 else others[by - 1][i * tall : (i + 1) * tall, :]
             at = pl.multiple_of(lax.rem(at_ref[0] + by, cols) * width, width)
-            term = dot(part[here, :], factor_ref[pl.ds(at, width), :])
+            term = dot(part, factor[pl.ds(at, width), :])
             total = term if total is None else total + term
-        out_ref[here, :] = total.astype(BF16)
-        return carry
-
-    lax.fori_loop(0, rows // tall, one, 0)
+        block[i] = total.astype(BF16)
+        store(i).start()
+    for i in range(tiles):
+        store(i).wait()
 
 
 def gather_rows(index, mapped_ref, loc):
@@ -125,7 +144,7 @@
     return dot(onehot, mapped_ref[...]).astype(BF16)
 
 
-def index_of(me, got, owners, cap, room, rows_dev):
+def decode(me, got, owners, cap, rows_dev):
     users = got.shape[0]
     pairs = owners * users
     lists, counts = got[:, :cap], got[:, cap : cap + pairs].astype(F32).astype(BF16)
@@ -134,17 +153,20 @@
     here = s == me
     count = dot(counts, bits(here & (w == lane)))
     start = dot(counts, bits(here & (w < lane)))
+    valid = iota((users, cap), 1) < start[:, users : users + 1].astype(I32)
+    to, row = div_mod(lists, rows_dev)
+    return jnp.where(valid, to, -1), row, count, start
+
+
+def index_of(me, got, owners, cap, room, rows_dev):
+    users = got.shape[0]
+    to, row, count, start = decode(me, got, owners, cap, rows_dev)
     earlier = bits(iota((users, users), 1) < iota((users, users), 0))
     delta = (dot(earlier, count.astype(BF16)) - start).astype(I32)
-    total = start[:, users : users + 1].astype(I32)
-    rank = iota((users, cap), 1)
-    valid = rank < total
-    to, row = div_mod(lists, rows_dev)
-    to = jnp.where(valid, to, -1)
-    pos = rank
+    pos = iota((users, cap), 1)
     for w in range(users):
         pos = pos + jnp.where(to == w, delta[:, w : w + 1], 0)
-    pos = jnp.where(valid, pos, -1)
+    pos = jnp.where(to >= 0, pos, -1)
     slot = iota((room, cap), 0)
     shard = iota((users, cap), 0)
     index = jnp.zeros((room, 2 * users), F32)
@@ -155,35 +177,134 @@
     return index[:, :users] + index[:, users:]
 
 
-def send_blocks(me, index_ref, mapped_ref, outs, block_ref, first):
-    users = index_ref.shape[2]
-
-    def one(i, carry):
-        group, loc = div_mod(me ^ (first + i), users)
-        block_ref[...] = gather_rows(index_ref[group], mapped_ref, loc)
+def send_set(me, mask, ranks_ref, mapped_ref, out_ref):
+    high = mapped_ref.shape[0] // 128
+    many = out_ref.shape[0]
+    tall = many // 4 if many % 64 == 0 else many
+    plane = div_mod(me, PLANE)[0] ^ mask
+    ranks = ranks_ref[pl.ds(pl.multiple_of(plane * high, high), high), :]
+
+    def one(t, carry):
+        slot = iota((tall, 128), 0) + t * tall
+        onehot = [bits(slot == ranks[h : h + 1, :]) for h in range(high)]
+        here = pl.ds(pl.multiple_of(t * tall, tall), tall)
+        out_ref[here, :] = dot(jnp.concatenate(onehot, axis=1), mapped_ref[...]).astype(BF16)
+        return carry
+
+    lax.fori_loop(0, many // tall, one, 0)
+
+
+def rank_kernel(me_ref, recv_ref, far_ref, ranks_ref, over_ref, out_ref, mapped_ref, done, *, users, cap, mask):
+    fetch = pltpu.make_async_copy(far_ref, mapped_ref, done.at[0])
+    fetch.start()
+    me = me_ref[0]
+    nearest = recv_ref.shape[0] // PLANE // 2
+    owners = recv_ref.shape[0]
+    rows_dev = mapped_ref.shape[0]
+    high = rows_dev // 128
+    planes = users // PLANE
+    total = planes * high
+    most = jnp.zeros((1, 1), F32)
+    for g in range(owners // users):
+        got = recv_ref[g * users : (g + 1) * users, 0, :]
+        to, row, _, _ = decode(me, got, owners, cap, rows_dev)
+        key = jnp.where(to >= 0, div_mod(to, PLANE)[0] * high + div_mod(row, 128)[0], -1)
+        low = div_mod(row, 128)[1]
+        left = [bits(iota((total, cap), 0) == key[u : u + 1, :]) for u in range(users)]
+        right = [bits(iota((128, cap), 0) == low[u : u + 1, :]) for u in range(users)]
+        seen = dot_nt(jnp.concatenate(left, axis=1), jnp.concatenate(right, axis=1))
+        present = bits(seen > 0.0)
+        within = dot(present, bits(iota((128, 128), 0) < iota((128, 128), 1)))
+        sums = dot(present, jnp.ones((128, 128), BF16)).astype(BF16)
+        pi, hi = div_mod(iota((total, total), 0), high)
+        pj, hj = div_mod(iota((total, total), 1), high)
+        rank = within + dot(bits((pi == pj) & (hj < hi)), sums)
+        ranks_ref[g * total : (g + 1) * total, :] = jnp.where(seen > 0.0, rank, -1.0).astype(I32)
+        whole = dot(bits(pi == pj), sums)
+        plane = div_mod(iota((total, 128), 0), high)[0] + g * planes
+        other = jnp.where((plane ^ div_mod(me, PLANE)[0]) < nearest, 0.0, whole)
+        most = jnp.maximum(most, jnp.max(jnp.max(other, axis=1, keepdims=True), axis=0, keepdims=True))
+    over_ref[...] = jnp.broadcast_to(jnp.where(most > out_ref.shape[0], 1.0, 0.0), over_ref.shape)
+    fetch.wait()
+    send_set(me, mask, ranks_ref, mapped_ref, out_ref)
+
+
+def index_kernel(me_ref, recv_ref, ranks_ref, over_ref, index_ref, *outs, masks, cap, rows_dev):
+    me = me_ref[0]
+    groups, room, users = index_ref.shape
+    wide = outs[0].shape[1]
+    high = rows_dev // 128
+    for g in range(groups):
+        got = recv_ref[g * users : (g + 1) * users, 0, :]
+        index_ref[g] = index_of(me, got, recv_ref.shape[0], cap, room, rows_dev)
+    same = iota((room, wide), 0) == iota((room, wide), 1)
+    for mask, out_ref in zip(masks, outs):
+        plane = div_mod(me, PLANE)[0] ^ mask
+        out_ref[...] = jnp.broadcast_to(over_ref[0:1, 0:1], out_ref.shape)
+        ranks = ranks_ref[pl.ds(pl.multiple_of(plane * high, high), high), :]
+
+        def one(j, carry, out_ref=out_ref, plane=plane, ranks=ranks):
+            group, loc = div_mod(plane * PLANE + j, users)
+            index = index_ref[group]
+            column = jnp.sum(jnp.where(iota(index.shape, 1) == loc, index, 0.0), axis=1, keepdims=True).astype(I32)
+            found = jnp.zeros((room, 128), I32)
+            for h in range(high):
+                found = jnp.where(iota((room, 128), 1) + 128 * h == column, ranks[h : h + 1, :], found)
+            place = jnp.sum(found.astype(F32), axis=1, keepdims=True)
+            out_ref[pl.ds(j, 1), :] = jnp.sum(jnp.where(same, place, 0.0), axis=0, keepdims=True)
+            return carry
+
+        lax.fori_loop(0, PLANE, one, 0)
+
+
+def sets_kernel(me_ref, ranks_ref, mapped_ref, after_ref, order_ref, *outs, masks):
+    for mask, out_ref in zip(masks, outs):
+        send_set(me_ref[0], mask, ranks_ref, mapped_ref, out_ref)
+    order_ref[...] = jnp.zeros(order_ref.shape, F32)
+
+
+def store_each(one, outs, block_ref):
+    def step(i, carry):
+        block_ref[...] = one(i)
         for k, out_ref in enumerate(outs):
             @pl.when(i == k)
             def _(out_ref=out_ref):
                 out_ref[...] = block_ref[...]
         return carry
 
-    lax.fori_loop(0, len(outs), one, 0)
-
-
-def index_kernel(me_ref, recv_ref, mapped_ref, index_ref, *refs, first, cap):
-    groups, room, users = index_ref.shape
-    for g in range(groups):
-        got = recv_ref[g * users : (g + 1) * users, 0, :]
-        index_ref[g] = index_of(me_ref[0], got, recv_ref.shape[0], cap, room, mapped_ref.shape[0])
-    send_blocks(me_ref[0], index_ref, mapped_ref, refs[:-1], refs[-1], first)
-
-
-def gather_kernel(me_ref, index_ref, mapped_ref, after_ref, order_ref, *refs, first):
-    send_blocks(me_ref[0], index_ref, mapped_ref, refs[:-1], refs[-1], first)
+    lax.fori_loop(0, len(outs), step, 0)
+
+
+def near_kernel(me_ref, index_ref, mapped_ref, after_ref, order_ref, *refs, first):
+    users = index_ref.shape[2]
+
+    def one(i):
+        group, loc = div_mod(me_ref[0] ^ (first + i), users)
+        return gather_rows(index_ref[group], mapped_ref, loc)
+
+    store_each(one, refs[:-1], refs[-1])
     order_ref[...] = jnp.zeros(order_ref.shape, F32)
 
 
-def meta_kernel(me_ref, recv_ref, seed_ref, user_ref, *, users, hist, rows_dev, seeds):
+def relay_kernel(me_ref, set_ref, places_ref, after_ref, order_ref, *refs, first):
+    many = set_ref.shape[0]
+    wide = places_ref.shape[1]
+    room = refs[-1].shape[0]
+    same = iota((room, wide), 0) == iota((room, wide), 1)
+    over = places_ref[PLANE : PLANE + 1, 0:1]
+
+    def one(i):
+        j = div_mod(me_ref[0] ^ (first + i), PLANE)[1]
+        column = jnp.sum(jnp.where(same, places_ref[pl.ds(j, 1), :], 0.0), axis=1, keepdims=True).astype(I32)
+        onehot = bits(iota((room, many), 1) == column)
+        got = dot(onehot, set_ref[...])
+        return jnp.where(iota(got.shape, 0) == room - 1, over, got).astype(BF16)
+
+    store_each(one, refs[:-1], refs[-1])
+    order_ref[...] = jnp.zeros(order_ref.shape, F32)
+
+
+def meta_kernel(me_ref, recv_ref, after_ref, seed_ref, user_ref, order_ref, *, users, hist, rows_dev, seeds):
     owners, room = seed_ref.shape
     group = pl.multiple_of(div_mod(me_ref[0], users)[0] * users, users)
     meta = recv_ref[pl.ds(group, users), 0, recv_ref.shape[2] - hist :]
@@ -198,6 +319,7 @@
         mine = shard == owner[u : u + 1, :]
         both = jnp.concatenate([jnp.where(mine, seed[u : u + 1, :].astype(F32), 0.0), jnp.where(mine, u + 1.0, 0.0)], axis=0)
         found = found + dot_nt(both.astype(BF16), onehot)
+    order_ref[...] = jnp.zeros(order_ref.shape, F32)
     seed_ref[...] = found[:owners].astype(I32)
     user_ref[...] = found[owners:].astype(I32)
 
@@ -248,7 +370,7 @@
 
 
 def first_kernel(*refs, owners):
-    rows_refs, (seed_ref, user_ref, table_ref, logits_ref, sent_ref, summed_ref) = refs[:owners], refs[owners:]
+    rows_refs, (seed_ref, user_ref, table_ref, logits_ref, sent_ref, summed_ref, flag_ref) = refs[:owners], refs[owners:]
     caps, seeds = table_ref.shape
     room = rows_refs[0].shape[0]
 
@@ -256,6 +378,8 @@
         onehot = jnp.where(iota((seeds, room), 0) == seed_ref[s : s + 1, :], 1.0, 0.0)
         return jnp.dot(table_ref[...], onehot, precision=lax.Precision.HIGHEST, preferred_element_type=F32)
 
+    flags = sum(ref[room - 16 :, :128].astype(F32) for ref in rows_refs[owners // 2 :])[15:]
+    flag_ref[...] = jnp.broadcast_to(flags, flag_ref.shape)
     route(initial, rows_refs, user_ref, summed_ref, logits_ref)
     products(rows_refs, user_ref, summed_ref, sent_ref, caps)
 
@@ -285,19 +409,20 @@
         products(rows_refs, user_ref, summed_ref, sent_ref, caps)
 
 
-def squash_kernel(summed_ref, *refs):
+def squash_kernel(summed_ref, flag_ref, *refs):
     scale = squash_scale(sum(part[:, :1] for part in refs[:-1]))
+    scale = jnp.where(flag_ref[0:1, 0:1] > 0.0, jnp.nan, scale)
     refs[-1][...] = summed_ref[...] * scale
 
 
-def call(kernel, out_shape, n_in, smem=(), flops=0, mib=16, **kw):
-    ins = [SMEM if i in smem else VMEM for i in range(n_in)]
+def call(kernel, out_shape, n_in, smem=(), far=(), far_out=False, flops=0, mib=12, **kw):
+    ins = [SMEM if i in smem else FAR if i in far else VMEM for i in range(n_in)]
     size = sum(math.prod(leaf.shape) * leaf.dtype.itemsize for leaf in jax.tree.leaves(out_shape))
     return pl.pallas_call(
         kernel,
         out_shape=out_shape,
         in_specs=ins,
-        out_specs=jax.tree.map(lambda _: VMEM, out_shape),
+        out_specs=jax.tree.map(lambda _: FAR if far_out else VMEM, out_shape),
         compiler_params=pltpu.CompilerParams(vmem_limit_bytes=mib << 20),
         cost_estimate=pl.CostEstimate(flops=flops, bytes_accessed=size, transcendentals=0),
         **kw,
@@ -353,9 +478,30 @@
     return summed * scale[:, :, None]
 
 
-def cuts_of(owners):
-    far = owners // 2
-    return [(far, far + 1), (far + 1, far + 4), (far + 4, owners), (0, far)]
+def map_table(factor, parts):
+    rows_dev, width = parts[0].shape
+    half = factor.shape[1]
+    tiles = 4
+    return call(
+        functools.partial(map_kernel, cols=len(parts)),
+        pltpu.HBM((rows_dev, half), BF16),
+        2 + len(parts),
+        smem=(0,),
+        far=(1, 2),
+        far_out=True,
+        flops=2 * rows_dev * half * factor.shape[0],
+        scratch_shapes=[
+            pltpu.VMEM(factor.shape, BF16),
+            pltpu.VMEM((tiles, rows_dev // tiles, width), BF16),
+            pltpu.VMEM((tiles, rows_dev // tiles, half), BF16),
+            pltpu.SemaphoreType.DMA((2 * tiles + 1,)),
+        ],
+    )(lax.axis_index("cols").reshape(1), factor, *parts)
+
+
+def plane_masks(owners):
+    planes = owners // PLANE
+    return list(range(planes // 2, planes))
 
 
 def on_device(item_ids, lengths, seed_rows, item_table, bilinear, seed_table):
@@ -372,6 +518,7 @@
     pairs = owners * users
     lanes = users * caps
     assert owners % users == 0 and owners & (owners - 1) == 0
+    assert users % PLANE == 0 and rows_dev % 128 == 0
     assert hist <= 256 and seeds <= 256 and rows_dev * users <= 65536
     local = lax.rem(me, users)
     group = me - local
@@ -385,80 +532,125 @@
         smem=(0,),
     )(local.reshape(1), item_ids, seed_rows, lengths.reshape(1, users))
     recv = lax.all_to_all(blocks, "users", split_axis=0, concat_axis=0, tiled=True)
-    mapped_rows = call(
-        functools.partial(map_kernel, cols=cols),
-        jax.ShapeDtypeStruct((rows_dev, half), BF16),
-        2 + cols,
+    mapped_rows = map_table(bilinear, table_parts)
+    counts = recv[:, 0, cap : cap + pairs].reshape(owners // users, users, pairs)
+    fits = jnp.max(jnp.sum(counts, axis=1)) < room
+
+    block = jax.ShapeDtypeStruct((room, half), BF16)
+    many = -(-PLANE * room * 11 // 15 // 64) * 64
+    one_set = jax.ShapeDtypeStruct((many, half), BF16)
+    wide = -(-room // 128) * 128
+    mark = jax.ShapeDtypeStruct((8, 128), F32)
+    groups = owners // users
+    planes = owners // PLANE
+    high = rows_dev // 128
+    scratch = [pltpu.VMEM((room, half), BF16)]
+    set_flops = 2 * many * half * rows_dev
+
+    def send(x, mask):
+        return lax.ppermute(x, "users", [(i, i ^ mask) for i in range(owners)])
+
+    masks = plane_masks(owners)
+    ranks, over, ready, mapped_rows = call(
+        functools.partial(rank_kernel, users=users, cap=cap, mask=masks[0]),
+        (jax.ShapeDtypeStruct((planes * high, 128), I32), mark, one_set, jax.ShapeDtypeStruct(mapped_rows.shape, BF16)),
+        3,
         smem=(0,),
-        flops=2 * rows_dev * half * bilinear.shape[0],
-    )(lax.axis_index("cols").reshape(1), bilinear, *table_parts)
-    counts = recv[:, 0, cap : cap + pairs].reshape(owners // users, users, pairs)
-    fits = jnp.max(jnp.sum(counts, axis=1)) <= room
-
-    block = jax.ShapeDtypeStruct((room, half), BF16)
-    scratch = [pltpu.VMEM((room, half), BF16)]
-    each = 2 * room * half * rows_dev
+        far=(2,),
+        flops=set_flops,
+        scratch_shapes=[pltpu.SemaphoreType.DMA((1,))],
+    )(here, recv, pltpu.with_memory_space_constraint(mapped_rows, pltpu.HBM))
+    sets = {masks[0]: send(ready, masks[0] * PLANE)}
+
+    def make_sets(chosen, after):
+        order, *ready = call(
+            functools.partial(sets_kernel, masks=chosen),
+            [mark] + [one_set] * len(chosen),
+            4,
+            smem=(0,),
+            flops=set_flops * len(chosen),
+        )(here, ranks, mapped_rows, after)
+        sets.update({mask: send(x, mask * PLANE) for mask, x in zip(chosen, ready)})
+        return order
+
+    index, *places = call(
+        functools.partial(index_kernel, masks=masks, cap=cap, rows_dev=rows_dev),
+        [jax.ShapeDtypeStruct((groups, room, users), F32)] + [jax.ShapeDtypeStruct((8, wide), F32)] * len(masks),
+        4,
+        smem=(0,),
+        flops=set_flops,
+    )(here, recv, ranks, over)
+    places = [send(x, mask * PLANE) for mask, x in zip(masks, places)]
     rows = [None] * owners
-    cuts = cuts_of(owners)
-    index = order = None
-    for first, stop in cuts:
-        many = stop - first
-        if index is None:
-            index, *sends = call(
-                functools.partial(index_kernel, first=first, cap=cap),
-                [jax.ShapeDtypeStruct((owners // users, room, users), F32)] + [block] * many,
-                3,
-                smem=(0,),
-                flops=many * each,
-                scratch_shapes=scratch,
-            )(here, recv, mapped_rows)
-            order = index
-        else:
-            order, *sends = call(
-                functools.partial(gather_kernel, first=first),
-                [jax.ShapeDtypeStruct((8, 128), F32)] + [block] * many,
+
+    def near(first, stop, order):
+        order, *blocks_out = call(
+            functools.partial(near_kernel, first=first),
+            [mark] + [block] * (stop - first),
+            4,
+            smem=(0,),
+            flops=2 * (stop - first) * room * half * rows_dev,
+            scratch_shapes=scratch,
+        )(here, index, mapped_rows, order)
+        for i, out in zip(range(first, stop), blocks_out):
+            rows[i] = send(out, i) if i else out
+        return order
+
+    order = near(PLANE, owners // 2, index)
+    order = near(0, PLANE, order)
+    where = jax.ShapeDtypeStruct((owners, room), I32)
+    seed, user, order = call(
+        functools.partial(meta_kernel, users=users, hist=hist, rows_dev=rows_dev, seeds=seeds), (where, where, mark), 3, smem=(0,)
+    )(here, recv, order)
+    order = make_sets(masks[1:], order)
+    for mask, place in zip(masks, places):
+        got = sets[mask]
+        for first, stop in RELAYS:
+            order, *blocks_out = call(
+                functools.partial(relay_kernel, first=first),
+                [mark] + [block] * (stop - first),
                 4,
                 smem=(0,),
-                flops=many * each,
+                flops=2 * (stop - first) * room * half * many,
                 scratch_shapes=scratch,
-            )(here, index, mapped_rows, order)
-        for mask, out in zip(range(first, stop), sends):
-            rows[mask] = out if mask == 0 else lax.ppermute(out, "users", [(i, i ^ mask) for i in range(owners)])
-
-    where = jax.ShapeDtypeStruct((owners, room), I32)
-    seed, user = call(
-        functools.partial(meta_kernel, users=users, hist=hist, rows_dev=rows_dev, seeds=seeds), (where, where), 2, smem=(0,)
-    )(here, recv)
+            )(here, got, place, order)
+            for i, out in zip(range(first, stop), blocks_out):
+                rows[mask * PLANE + i] = send(out, i) if i else out
+
     logits_shape = jax.ShapeDtypeStruct((owners, caps, room), F32)
-    wide = (room // 128 + 1) * 128
-    sent_shape = jax.ShapeDtypeStruct((owners * caps, wide), F32)
+    sent_shape = jax.ShapeDtypeStruct((owners * caps, (room // 128 + 1) * 128), F32)
     summed_shape = jax.ShapeDtypeStruct((lanes, half), F32)
     square_shape = jax.ShapeDtypeStruct((lanes, 128), F32)
     step_shapes = (logits_shape, sent_shape, summed_shape)
     kernel = functools.partial(first_kernel, owners=owners)
-    logits, sent, _ = call(kernel, step_shapes, owners + 3)(*rows, seed, user, seed_table.T)
+    logits, sent, _, flag = call(kernel, step_shapes + (mark,), owners + 3)(*rows, seed, user, seed_table.T)
     later = functools.partial(later_kernel, cols=cols, owners=owners, lanes=lanes)
     for _ in range(ITERS - 2):
         kernel = functools.partial(later, last=False)
         logits, sent, _ = call(kernel, step_shapes, cols + owners + 2)(*all_cols(sent), *rows, user, logits)
     kernel = functools.partial(later, last=True)
     summed, square = call(kernel, (summed_shape, square_shape), cols + owners + 2)(*all_cols(sent), *rows, user, logits)
-    capsules = call(squash_kernel, summed_shape, cols + 1)(summed, *all_cols(square)).reshape(users, caps, half)
+    capsules = call(squash_kernel, summed_shape, cols + 2)(summed, flag, *all_cols(square)).reshape(users, caps, half)
     if owners > users:
         spread = jnp.zeros((owners, caps, half), F32)
         capsules = lax.dynamic_update_slice_in_dim(spread, capsules, group, 0)
     back = lax.all_to_all(capsules, "users", split_axis=0, concat_axis=0, tiled=True)
     if owners > users:
         back = lax.dynamic_slice_in_dim(back, group, users, 0)
+    over = jnp.max(jnp.where(jnp.isnan(back[:, 0, 0]), 1, 0))
+    if owners > users:
+        over = lax.pmax(over, "users")
+    fits = fits & (over == 0)
     dealt = back[dest[:, 0]]
 
     def kept(dealt, *_):
         return dealt
 
-    def full(dealt, mapped_rows, seed_table, item_ids, lengths, seed_rows):
+    def full(dealt, item_table, bilinear, seed_table, item_ids, lengths, seed_rows):
+        mapped_rows = map_table(bilinear, all_cols(item_table))
         return any_input(item_ids, lengths, seed_rows, mapped_rows, seed_table, cap)
 
-    return lax.cond(fits, kept, full, dealt, mapped_rows, seed_table, item_ids, lengths, seed_rows)
+    return lax.cond(fits, kept, full, dealt, item_table, bilinear, seed_table, item_ids, lengths, seed_rows)
 
 
 def solution(mesh):

time: 174 us -> 175 us (level)
  waiting for transfers between devices: 50.4 us -> 95.2 us
  starting transfers between devices: 82.2 us -> 37.8 us
  local copies, waits for them, and re-layouts: 4.18 us -> 1.36 us
  Pallas kernels: 34.9 us -> 37.5 us
    ppermute x15 -> x17, starting transfers between devices: 68.7 us -> 24.5 us  [send(): return lax.ppermute(x, 'users', [(i, i ^ mask) for i in range(owners)])]
    ppermute x15 -> x17, waiting for transfers between devices: 37.9 us -> 80.3 us  [send(): return lax.ppermute(x, 'users', [(i, i ^ mask) for i in range(owners)])]
    unnamed x16 -> x10, local copies, waits for them, and re-layouts: 3.53 us -> 0.71 us
    pallas_call x7 -> x14, Pallas kernels: 27.1 us -> 29.5 us  [the longest x2 6.02 us: near(): call(functools.partial(near_kernel, first=first), [mark] + [block] * (sto...]
    all_to_all x1, waiting for transfers between devices: 0.01 us -> 2.43 us  [on_device(): lax.all_to_all(blocks, 'users', split_axis=0, concat_axis=0, tiled=True)]
  transfers between devices with their start and end apart: 21 -> 23, of which waited for: 12 -> 14; matrix products, arithmetic and copies ran while one was open for 0% -> 0% of each run, Pallas kernels for 5% -> 9%
where the time goes in v3:
time: 175 us
  waiting for transfers between devices  95.2 us (54%)
  starting transfers between devices  37.8 us (22%)
  Pallas kernels  37.5 us (21%)
    ppermute x17, waiting for transfers between devices, send(): return lax.ppermute(x, 'users', [(i, i ^ mask) for i in range(owners)])  80.3 us
    ppermute x17, starting transfers between devices, send(): return lax.ppermute(x, 'users', [(i, i ^ mask) for i in range(owners)])  24.5 us
    all_to_all x1, waiting for transfers between devices, on_device(): lax.all_to_all(capsules, 'users', split_axis=0, concat_axis=0, tiled=True)  8.86 us
    all_to_all x1, starting transfers between devices, on_device(): lax.all_to_all(blocks, 'users', split_axis=0, concat_axis=0, tiled=True)  7.85 us
    pallas_call x2, Pallas kernels, near(): call(functools.partial(near_kernel, first=first), [mark] + [block] * (sto...  6.02 us
    pallas_call x1, Pallas kernels, map_table(): call(functools.partial(map_kernel, cols=len(parts)), pltpu.HBM((rows_dev,...  5.08 us
    pallas_call x1, Pallas kernels, on_device(): call(functools.partial(index_kernel, masks=masks, cap=cap, rows_dev=rows_...  4.58 us
    all_to_all x1, starting transfers between devices, on_device(): lax.all_to_all(capsules, 'users', split_axis=0, concat_axis=0, tiled=True)  4.45 us
  transfers between devices with their start and end apart: 23, of which 14 were waited for; matrix products, arithmetic and copies ran while one was open for 0% of the time, Pallas kernels for 9%

profile of v3, /device:TPU:0, one launch (start us, length us, event | category | flops | bytes accessed | tf_op | source)
XLA Modules:
  0.0 174.7 jit_solution(8848320891971642321)
XLA Ops:
  0.5 3.4 %shard_map.66 = (s32[16,1,1024]{2,1,0:T(1,128)}, s32[16,1]{1,0:T(8,128)S(1)}) custom-call(s32[1]{0:T(128)} %bitcast.12.local_ref, s32[16,256]{1,0:T(8,128)} %ids_ref.1, s32[16,256]{1,0:T(8,128)} %seeds_ref.1, s32[1,16]{1,0:T(1,128)} %bitcast.68), custom_call_target="tpu_custom_call" | custom-call | bytes 65600 | tf_op jit(solution)/shard_map/pallas_call | solution.py:528
  3.9 7.9 %all-to-all-start.2 = ((s32[16,1,1024]{2,1,0:T(1,128)}), s32[16,1,1024]{2,1,0:T(1,128)S(1)}, u32[]{:S(2)}, u32[]{:S(2)}) async-start(s32[16,1,1024]{2,1,0:T(1,128)} %get-tuple-element.87), calls=%async_computation.2 | async-start | bytes 131072 | tf_op jit(solution)/shard_map/all_to_all | solution.py:534
  11.7 5.1 %shard_map.67.far_ref = bf16[2048,512]{1,0:T(8,128)(2,1)} custom-call(s32[1]{0:T(128)} %bitcast.15.refs_0_, bf16[1024,512]{1,0:T(8,128)(2,1)} %refs_1_.1, bf16[2048,512]{1,0:T(8,128)(2,1)} %refs_2_.1, bf16[2048,512]{1,0:T(8,128)(2,1)S(1)} %collective-permute-done.6.refs_3_), custom_call_target="tpu_custom_call" | custom-call | flops 2147483648 | bytes 2097152 | tf_op jit(solution)/shard_map/pallas_call | solution.py:485
  16.8 2.4 %all-to-all-done.2.recv_ref = s32[16,1,1024]{2,1,0:T(1,128)S(1)} async-done(((s32[16,1,1024]{2,1,0:T(1,128)}), s32[16,1,1024]{2,1,0:T(1,128)S(1)}, u32[]{:S(2)}, u32[]{:S(2)}) %all-to-all-start.2) | async-done | bytes 65568 | tf_op jit(solution)/shard_map/all_to_all | solution.py:534
  19.3 3.8 %shard_map.68 = (s32[64,128]{1,0:T(8,128)S(1)}, f32[8,128]{1,0:T(8,128)S(1)}, bf16[704,512]{1,0:T(8,128)(2,1)S(1)}, bf16[2048,512]{1,0:T(8,128)(2,1)S(1)}) custom-call(s32[1]{0:T(128)} %bitcast.14.me_ref, s32[16,1,1024]{2,1,0:T(1,128)S(1)} %all-to-all-done.2.recv_ref, bf16[2048,512]{1,0:T(8,128)(2,1)} %shard_map.67.far_ref), custom_call_target="tpu_custom_call" | custom-call | flops 1476395008 | bytes 2854912 | tf_op jit(solution)/shard_map/pallas_call | solution.py:554
  23.0 4.6 %shard_map.69 = (f32[1,240,16]{2,1,0:T(8,128)S(1)}, f32[8,256]{1,0:T(8,128)S(1)}, f32[8,256]{1,0:T(8,128)S(1)}) custom-call(s32[1]{0:T(128)} %bitcast.14.me_ref, s32[16,1,1024]{2,1,0:T(1,128)S(1)} %all-to-all-done.2.recv_ref, s32[64,128]{1,0:T(8,128)S(1)} %get-tuple-element.88.ranks_ref, f32[8,128]{1,0:T(8,128)S(1)} %get-tuple-element.89.over_ref), custom_call_target="tpu_custom_call" | custom-call | flops 1476395008 | bytes 31744 | tf_op jit(solution)/shard_map/pallas_call | solution.py:576
  27.6 3.0 %shard_map.70 = (f32[8,128]{1,0:T(8,128)S(1)}, bf16[240,512]{1,0:T(8,128)(2,1)S(1)}, bf16[240,512]{1,0:T(8,128)(2,1)S(1)}, bf16[240,512]{1,0:T(8,128)(2,1)S(1)}, bf16[240,512]{1,0:T(8,128)(2,1)S(1)}) custom-call(s32[1]{0:T(128)} %bitcast.14.me_ref, f32[1,240,16]{2,1,0:T(8,128)S(1)} %get-tuple-element.90.index_ref.after_ref, ...), custom_call_target="tpu_custom_call" | custom-call | flops 2013265920 | bytes 987136 | tf_op jit(solution)/shard_map/pallas_call | solution.py:587
  30.7 3.0 %shard_map.71 = (f32[8,128]{1,0:T(8,128)S(1)}, bf16[240,512]{1,0:T(8,128)(2,1)S(1)}, bf16[240,512]{1,0:T(8,128)(2,1)S(1)}, bf16[240,512]{1,0:T(8,128)(2,1)S(1)}, bf16[240,512]{1,0:T(8,128)(2,1)S(1)}) custom-call(s32[1]{0:T(128)} %bitcast.14.me_ref, f32[1,240,16]{2,1,0:T(8,128)S(1)} %get-tuple-element.90.index_ref.after_ref, ...), custom_call_target="tpu_custom_call" | custom-call | flops 2013265920 | bytes 987136 | tf_op jit(solution)/shard_map/pallas_call | solution.py:587
  34.5 1.3 shard_map.72
  35.8 2.2 %shard_map.73 = (f32[8,128]{1,0:T(8,128)S(1)}, bf16[704,512]{1,0:T(8,128)(2,1)S(1)}) custom-call(s32[1]{0:T(128)} %bitcast.14.me_ref, s32[64,128]{1,0:T(8,128)S(1)} %get-tuple-element.88.ranks_ref, bf16[2048,512]{1,0:T(8,128)(2,1)S(1)} %get-tuple-element.91.mapped_ref, f32[8,128]{1,0:T(8,128)S(1)} %get-tuple-element.104.after_ref), custom_call_target="tpu_custom_call" | custom-call | flops 1476395008 | bytes 724992 | tf_op jit(solution)/shard_map/pallas_call | solution.py:566
  38.0 2.3 %collective-permute-start.19 = (bf16[704,512]{1,0:T(8,128)(2,1)S(1)}, bf16[704,512]{1,0:T(8,128)(2,1)S(1)}, u32[]{:S(2)}, u32[]{:S(2)}) collective-permute-start(bf16[704,512]{1,0:T(8,128)(2,1)S(1)} %get-tuple-element.112), channel_id=1, source_target_pairs={{0,24},{2,26},{4,28},{6,30},{8,16},{10,18},{12,20},{14,22},{16,8},... | collective-permute-start | bytes 2162696 | tf_op jit(solution)/shard_map/ppermute | solution.py:551
  40.7 1.5 collective-permute-start.7
  42.1 1.5 collective-permute-start.8
  43.6 54.9 %collective-permute-done.15.places_ref = f32[8,256]{1,0:T(8,128)S(1)} collective-permute-done((f32[8,256]{1,0:T(8,128)S(1)}, f32[8,256]{1,0:T(8,128)S(1)}, u32[]{:S(2)}, u32[]{:S(2)}) %collective-permute-start.15) | collective-permute-done | bytes 8224 | tf_op jit(solution)/shard_map/ppermute | solution.py:551
  98.5 1.3 collective-permute-start.9
  99.7 3.3 %collective-permute-start.20 = (f32[8,256]{1,0:T(8,128)S(1)}, f32[8,256]{1,0:T(8,128)S(1)}, u32[]{:S(2)}, u32[]{:S(2)}) collective-permute-start(f32[8,256]{1,0:T(8,128)S(1)} %get-tuple-element.113), channel_id=1, source_target_pairs={{0,24},{2,26},{4,28},{6,30},{8,16},{10,18},{12,20},{14,22},{16,8},... | collective-permute-start | bytes 24584 | tf_op jit(solution)/shard_map/ppermute | solution.py:551
  105.2 2.6 %collective-permute-start.11 = (bf16[240,512]{1,0:T(8,128)(2,1)S(1)}, bf16[240,512]{1,0:T(8,128)(2,1)S(1)}, u32[]{:S(2)}, u32[]{:S(2)}) collective-permute-start(bf16[240,512]{1,0:T(8,128)(2,1)S(1)} %get-tuple-element.98), channel_id=1, source_target_pairs={{0,10},{2,8},{4,14},{6,12},{8,2},{10,0},{12,6},{14,4},{16,26},{18,... | collective-permute-start | bytes 737288 | tf_op jit(solution)/shard_map/ppermute | solution.py:551
  110.0 2.7 %collective-permute-start.13 = (bf16[240,512]{1,0:T(8,128)(2,1)S(1)}, bf16[240,512]{1,0:T(8,128)(2,1)S(1)}, u32[]{:S(2)}, u32[]{:S(2)}) collective-permute-start(bf16[240,512]{1,0:T(8,128)(2,1)S(1)} %get-tuple-element.100), channel_id=1, source_target_pairs={{0,14},{2,12},{4,10},{6,8},{8,6},{10,4},{12,2},{14,0},{16,30},{18,... | collective-permute-start | bytes 737288 | tf_op jit(solution)/shard_map/ppermute | solution.py:551
  114.0 1.7 collective-permute-start.23
  115.7 4.1 %collective-permute-done.11.refs_5_.refs_7_ = bf16[240,512]{1,0:T(8,128)(2,1)S(1)} collective-permute-done((bf16[240,512]{1,0:T(8,128)(2,1)S(1)}, bf16[240,512]{1,0:T(8,128)(2,1)S(1)}, u32[]{:S(2)}, u32[]{:S(2)}) %collective-permute-start.11) | collective-permute-done | bytes 245792 | tf_op jit(solution)/shard_map/ppermute | solution.py:551
  120.8 5.1 %collective-permute-done.12.refs_6_.refs_8_ = bf16[240,512]{1,0:T(8,128)(2,1)S(1)} collective-permute-done((bf16[240,512]{1,0:T(8,128)(2,1)S(1)}, bf16[240,512]{1,0:T(8,128)(2,1)S(1)}, u32[]{:S(2)}, u32[]{:S(2)}) %collective-permute-start.12) | collective-permute-done | bytes 245792 | tf_op jit(solution)/shard_map/ppermute | solution.py:551
  127.1 1.7 %collective-permute-done.13.refs_7_.refs_9_ = bf16[240,512]{1,0:T(8,128)(2,1)S(1)} collective-permute-done((bf16[240,512]{1,0:T(8,128)(2,1)S(1)}, bf16[240,512]{1,0:T(8,128)(2,1)S(1)}, u32[]{:S(2)}, u32[]{:S(2)}) %collective-permute-start.13) | collective-permute-done | bytes 245792 | tf_op jit(solution)/shard_map/ppermute | solution.py:551
  128.8 2.0 %collective-permute-start.18 = (bf16[240,512]{1,0:T(8,128)(2,1)S(1)}, bf16[240,512]{1,0:T(8,128)(2,1)S(1)}, u32[]{:S(2)}, u32[]{:S(2)}) collective-permute-start(bf16[240,512]{1,0:T(8,128)(2,1)S(1)} %get-tuple-element.111), channel_id=1, source_target_pairs={{0,6},{2,4},{4,2},{6,0},{8,14},{10,12},{12,10},{14,8},{16,22},{18,... | collective-permute-start | bytes 737288 | tf_op jit(solution)/shard_map/ppermute | solution.py:551
  130.9 8.5 %collective-permute-done.22.refs_14_.refs_16_ = bf16[240,512]{1,0:T(8,128)(2,1)S(1)} collective-permute-done((bf16[240,512]{1,0:T(8,128)(2,1)S(1)}, bf16[240,512]{1,0:T(8,128)(2,1)S(1)}, u32[]{:S(2)}, u32[]{:S(2)}) %collective-permute-start.22) | collective-permute-done | bytes 245792 | tf_op jit(solution)/shard_map/ppermute | solution.py:551
  141.1 3.6 %collective-permute-done.17.refs_10_.refs_12_ = bf16[240,512]{1,0:T(8,128)(2,1)S(1)} collective-permute-done((bf16[240,512]{1,0:T(8,128)(2,1)S(1)}, bf16[240,512]{1,0:T(8,128)(2,1)S(1)}, u32[]{:S(2)}, u32[]{:S(2)}) %collective-permute-start.17) | collective-permute-done | bytes 245792 | tf_op jit(solution)/shard_map/ppermute | solution.py:551
  144.7 1.7 collective-permute-done.16.refs_9_.refs_11_
  146.3 2.8 %shard_map.80 = (f32[16,8,240]{2,1,0:T(8,128)S(1)}, f32[128,256]{1,0:T(8,128)S(1)}, f32[128,512]{1,0:T(8,128)}, f32[8,128]{1,0:T(8,128)S(1)}) custom-call(bf16[240,512]{1,0:T(8,128)(2,1)S(1)} %get-tuple-element.93.refs_0_.refs_2_, bf16[240,512]{1,0:T(8,128)(2,1)S(1)} %collective-permute-done.7.refs_1_.refs_3_, ...), custom_call_target="tpu_custom_call" | custom-call | bytes 520192 | tf_op jit(solution)/shard_map/pallas_call | solution.py:626
  149.2 1.3 collective-permute-done.24.refs_1_
  150.5 2.2 %shard_map.81 = (f32[16,8,240]{2,1,0:T(8,128)S(1)}, f32[128,256]{1,0:T(8,128)S(1)}, f32[128,512]{1,0:T(8,128)}) custom-call(f32[128,256]{1,0:T(8,128)S(1)} %get-tuple-element.123.refs_0_, f32[128,256]{1,0:T(8,128)S(1)} %collective-permute-done.24.refs_1_, bf16[240,512]{1,0:T(8,128)(2,1)S(1)} %get-tuple-element.93.refs_0_.refs_2_, ...), custom_call_target="tpu_custom_call" | custom-call | bytes 516096 | tf_op jit(solution)/shard_map/pallas_call | solution.py:630
  153.0 1.2 collective-permute-done.25.refs_1_
  157.4 4.4 %all-to-all-start.3 = ((f32[16,8,512]{2,1,0:T(8,128)}), f32[16,8,512]{2,1,0:T(8,128)S(1)}, u32[]{:S(2)}, u32[]{:S(2)}) async-start(f32[16,8,512]{2,1,0:T(8,128)} %bitcast.17), calls=%async_computation.3 | async-start | bytes 524288 | tf_op jit(solution)/shard_map/all_to_all | solution.py:637
  163.2 8.9 %all-to-all-done.3 = f32[16,8,512]{2,1,0:T(8,128)S(1)} async-done(((f32[16,8,512]{2,1,0:T(8,128)}), f32[16,8,512]{2,1,0:T(8,128)S(1)}, u32[]{:S(2)}, u32[]{:S(2)}) %all-to-all-start.3) | async-done | bytes 262176 | tf_op jit(solution)/shard_map/all_to_all | solution.py:637
  (50 shorter events, 18.0 us)
Async XLA Ops:
  0.0 11.7 %collective-permute-start.6 = (bf16[2048,512]{1,0:T(8,128)(2,1)}, bf16[2048,512]{1,0:T(8,128)(2,1)S(1)}, u32[]{:S(2)}, u32[]{:S(2)}) collective-permute-start(bf16[2048,512]{1,0:T(8,128)(2,1)} %refs_2_.1), channel_id=1, source_target_pairs={{1,0},{0,1},{3,2},{2,3},{5,4},{4,5},{7,6},{6,7},{9,8},{8,9},{11,10... | collective-permute-start | bytes 6291464 | tf_op jit(solution)/shard_map/ppermute | solution.py:434
  3.9 15.4 %all-to-all-start.2 = ((s32[16,1,1024]{2,1,0:T(1,128)}), s32[16,1,1024]{2,1,0:T(1,128)S(1)}, u32[]{:S(2)}, u32[]{:S(2)}) async-start(s32[16,1,1024]{2,1,0:T(1,128)} %get-tuple-element.87), calls=%async_computation.2 | async-start | bytes 131072 | tf_op jit(solution)/shard_map/all_to_all | solution.py:534
  33.7 66.1 %collective-permute-start.14 = (bf16[704,512]{1,0:T(8,128)(2,1)S(1)}, bf16[704,512]{1,0:T(8,128)(2,1)S(1)}, u32[]{:S(2)}, u32[]{:S(2)}) collective-permute-start(bf16[704,512]{1,0:T(8,128)(2,1)S(1)} %get-tuple-element.101), channel_id=1, source_target_pairs={{0,16},{2,18},{4,20},{6,22},{8,24},{10,26},{12,28},{14,30},{16,0},... | collective-permute-start | bytes 2162696 | tf_op jit(solution)/shard_map/ppermute | solution.py:551
  35.8 110.5 %copy-start.4 = (f32[64,8]{0,1:T(8,128)S(1)}, f32[64,8]{0,1:T(8,128)}, u32[]{:S(2)}) copy-start(f32[64,8]{0,1:T(8,128)} %param.13) | copy-start | bytes 6148
  38.0 67.2 %collective-permute-start.19 = (bf16[704,512]{1,0:T(8,128)(2,1)S(1)}, bf16[704,512]{1,0:T(8,128)(2,1)S(1)}, u32[]{:S(2)}, u32[]{:S(2)}) collective-permute-start(bf16[704,512]{1,0:T(8,128)(2,1)S(1)} %get-tuple-element.112), channel_id=1, source_target_pairs={{0,24},{2,26},{4,28},{6,30},{8,16},{10,18},{12,20},{14,22},{16,8},... | collective-permute-start | bytes 2162696 | tf_op jit(solution)/shard_map/ppermute | solution.py:551
  40.3 58.1 %collective-permute-start.15 = (f32[8,256]{1,0:T(8,128)S(1)}, f32[8,256]{1,0:T(8,128)S(1)}, u32[]{:S(2)}, u32[]{:S(2)}) collective-permute-start(f32[8,256]{1,0:T(8,128)S(1)} %get-tuple-element.102), channel_id=1, source_target_pairs={{0,16},{2,18},{4,20},{6,22},{8,24},{10,26},{12,28},{14,30},{16,0},... | collective-permute-start | bytes 24584 | tf_op jit(solution)/shard_map/ppermute | solution.py:551
  40.7 68.7 %collective-permute-start.7 = (bf16[240,512]{1,0:T(8,128)(2,1)S(1)}, bf16[240,512]{1,0:T(8,128)(2,1)S(1)}, u32[]{:S(2)}, u32[]{:S(2)}) collective-permute-start(bf16[240,512]{1,0:T(8,128)(2,1)S(1)} %get-tuple-element.94), channel_id=1, source_target_pairs={{0,2},{2,0},{4,6},{6,4},{8,10},{10,8},{12,14},{14,12},{16,18},{18,... | collective-permute-start | bytes 737288 | tf_op jit(solution)/shard_map/ppermute | solution.py:551
  42.1 67.8 %collective-permute-start.8 = (bf16[240,512]{1,0:T(8,128)(2,1)S(1)}, bf16[240,512]{1,0:T(8,128)(2,1)S(1)}, u32[]{:S(2)}, u32[]{:S(2)}) collective-permute-start(bf16[240,512]{1,0:T(8,128)(2,1)S(1)} %get-tuple-element.95), channel_id=1, source_target_pairs={{0,4},{2,6},{4,0},{6,2},{8,12},{10,14},{12,8},{14,10},{16,20},{18,... | collective-permute-start | bytes 737288 | tf_op jit(solution)/shard_map/ppermute | solution.py:551
  98.5 14.2 %collective-permute-start.9 = (bf16[240,512]{1,0:T(8,128)(2,1)S(1)}, bf16[240,512]{1,0:T(8,128)(2,1)S(1)}, u32[]{:S(2)}, u32[]{:S(2)}) collective-permute-start(bf16[240,512]{1,0:T(8,128)(2,1)S(1)} %get-tuple-element.96), channel_id=1, source_target_pairs={{0,6},{2,4},{4,2},{6,0},{8,14},{10,12},{12,10},{14,8},{16,22},{18,... | collective-permute-start | bytes 737288 | tf_op jit(solution)/shard_map/ppermute | solution.py:551
  99.7 5.4 %collective-permute-start.20 = (f32[8,256]{1,0:T(8,128)S(1)}, f32[8,256]{1,0:T(8,128)S(1)}, u32[]{:S(2)}, u32[]{:S(2)}) collective-permute-start(f32[8,256]{1,0:T(8,128)S(1)} %get-tuple-element.113), channel_id=1, source_target_pairs={{0,24},{2,26},{4,28},{6,30},{8,16},{10,18},{12,20},{14,22},{16,8},... | collective-permute-start | bytes 24584 | tf_op jit(solution)/shard_map/ppermute | solution.py:551
  105.2 8.8 %collective-permute-start.10 = (bf16[240,512]{1,0:T(8,128)(2,1)S(1)}, bf16[240,512]{1,0:T(8,128)(2,1)S(1)}, u32[]{:S(2)}, u32[]{:S(2)}) collective-permute-start(bf16[240,512]{1,0:T(8,128)(2,1)S(1)} %get-tuple-element.97), channel_id=1, source_target_pairs={{0,8},{2,10},{4,12},{6,14},{8,0},{10,2},{12,4},{14,6},{16,24},{18,... | collective-permute-start | bytes 737288 | tf_op jit(solution)/shard_map/ppermute | solution.py:551
  105.2 14.6 %collective-permute-start.11 = (bf16[240,512]{1,0:T(8,128)(2,1)S(1)}, bf16[240,512]{1,0:T(8,128)(2,1)S(1)}, u32[]{:S(2)}, u32[]{:S(2)}) collective-permute-start(bf16[240,512]{1,0:T(8,128)(2,1)S(1)} %get-tuple-element.98), channel_id=1, source_target_pairs={{0,10},{2,8},{4,14},{6,12},{8,2},{10,0},{12,6},{14,4},{16,26},{18,... | collective-permute-start | bytes 737288 | tf_op jit(solution)/shard_map/ppermute | solution.py:551
  109.3 16.6 %collective-permute-start.12 = (bf16[240,512]{1,0:T(8,128)(2,1)S(1)}, bf16[240,512]{1,0:T(8,128)(2,1)S(1)}, u32[]{:S(2)}, u32[]{:S(2)}) collective-permute-start(bf16[240,512]{1,0:T(8,128)(2,1)S(1)} %get-tuple-element.99), channel_id=1, source_target_pairs={{0,12},{2,14},{4,8},{6,10},{8,4},{10,6},{12,0},{14,2},{16,28},{18,... | collective-permute-start | bytes 737288 | tf_op jit(solution)/shard_map/ppermute | solution.py:551
  110.0 18.9 %collective-permute-start.13 = (bf16[240,512]{1,0:T(8,128)(2,1)S(1)}, bf16[240,512]{1,0:T(8,128)(2,1)S(1)}, u32[]{:S(2)}, u32[]{:S(2)}) collective-permute-start(bf16[240,512]{1,0:T(8,128)(2,1)S(1)} %get-tuple-element.100), channel_id=1, source_target_pairs={{0,14},{2,12},{4,10},{6,8},{8,6},{10,4},{12,2},{14,0},{16,30},{18,... | collective-permute-start | bytes 737288 | tf_op jit(solution)/shard_map/ppermute | solution.py:551
  112.7 26.7 %collective-permute-start.22 = (bf16[240,512]{1,0:T(8,128)(2,1)S(1)}, bf16[240,512]{1,0:T(8,128)(2,1)S(1)}, u32[]{:S(2)}, u32[]{:S(2)}) collective-permute-start(bf16[240,512]{1,0:T(8,128)(2,1)S(1)} %get-tuple-element.119), channel_id=1, source_target_pairs={{0,4},{2,6},{4,0},{6,2},{8,12},{10,14},{12,8},{14,10},{16,20},{18,... | collective-permute-start | bytes 737288 | tf_op jit(solution)/shard_map/ppermute | solution.py:551
  114.0 27.1 %collective-permute-start.23 = (bf16[240,512]{1,0:T(8,128)(2,1)S(1)}, bf16[240,512]{1,0:T(8,128)(2,1)S(1)}, u32[]{:S(2)}, u32[]{:S(2)}) collective-permute-start(bf16[240,512]{1,0:T(8,128)(2,1)S(1)} %get-tuple-element.120), channel_id=1, source_target_pairs={{0,6},{2,4},{4,2},{6,0},{8,14},{10,12},{12,10},{14,8},{16,22},{18,... | collective-permute-start | bytes 737288 | tf_op jit(solution)/shard_map/ppermute | solution.py:551
  119.8 21.3 %collective-permute-start.21 = (bf16[240,512]{1,0:T(8,128)(2,1)S(1)}, bf16[240,512]{1,0:T(8,128)(2,1)S(1)}, u32[]{:S(2)}, u32[]{:S(2)}) collective-permute-start(bf16[240,512]{1,0:T(8,128)(2,1)S(1)} %get-tuple-element.118), channel_id=1, source_target_pairs={{0,2},{2,0},{4,6},{6,4},{8,10},{10,8},{12,14},{14,12},{16,18},{18,... | collective-permute-start | bytes 737288 | tf_op jit(solution)/shard_map/ppermute | solution.py:551
  125.9 18.7 %collective-permute-start.17 = (bf16[240,512]{1,0:T(8,128)(2,1)S(1)}, bf16[240,512]{1,0:T(8,128)(2,1)S(1)}, u32[]{:S(2)}, u32[]{:S(2)}) collective-permute-start(bf16[240,512]{1,0:T(8,128)(2,1)S(1)} %get-tuple-element.110), channel_id=1, source_target_pairs={{0,4},{2,6},{4,0},{6,2},{8,12},{10,14},{12,8},{14,10},{16,20},{18,... | collective-permute-start | bytes 737288 | tf_op jit(solution)/shard_map/ppermute | solution.py:551
  128.8 15.8 %collective-permute-start.18 = (bf16[240,512]{1,0:T(8,128)(2,1)S(1)}, bf16[240,512]{1,0:T(8,128)(2,1)S(1)}, u32[]{:S(2)}, u32[]{:S(2)}) collective-permute-start(bf16[240,512]{1,0:T(8,128)(2,1)S(1)} %get-tuple-element.111), channel_id=1, source_target_pairs={{0,6},{2,4},{4,2},{6,0},{8,14},{10,12},{12,10},{14,8},{16,22},{18,... | collective-permute-start | bytes 737288 | tf_op jit(solution)/shard_map/ppermute | solution.py:551
  139.4 6.9 %collective-permute-start.16 = (bf16[240,512]{1,0:T(8,128)(2,1)S(1)}, bf16[240,512]{1,0:T(8,128)(2,1)S(1)}, u32[]{:S(2)}, u32[]{:S(2)}) collective-permute-start(bf16[240,512]{1,0:T(8,128)(2,1)S(1)} %get-tuple-element.109), channel_id=1, source_target_pairs={{0,2},{2,0},{4,6},{6,4},{8,10},{10,8},{12,14},{14,12},{16,18},{18,... | collective-permute-start | bytes 737288 | tf_op jit(solution)/shard_map/ppermute | solution.py:551
  149.1 1.3 collective-permute-start.24
  150.5 22.8 %copy-start.2 = (s32[16,256]{1,0:T(8,128)S(1)}, s32[16,256]{1,0:T(8,128)}, u32[]{:S(2)}) copy-start(s32[16,256]{1,0:T(8,128)} %ids_ref.1) | copy-start | bytes 49156
  150.5 22.8 %copy-start.3 = (s32[16,256]{1,0:T(8,128)S(1)}, s32[16,256]{1,0:T(8,128)}, u32[]{:S(2)}) copy-start(s32[16,256]{1,0:T(8,128)} %seeds_ref.1) | copy-start | bytes 49156
  150.5 22.8 %copy-start.5 = (s32[16]{0:T(128)S(1)}, s32[16]{0:T(128)}, u32[]{:S(2)}) copy-start(s32[16]{0:T(128)} %param.9) | copy-start | bytes 196
  152.8 1.4 collective-permute-start.25
  155.2 1.3 collective-permute-start.26
  157.4 14.6 %all-to-all-start.3 = ((f32[16,8,512]{2,1,0:T(8,128)}), f32[16,8,512]{2,1,0:T(8,128)S(1)}, u32[]{:S(2)}, u32[]{:S(2)}) async-start(f32[16,8,512]{2,1,0:T(8,128)} %bitcast.17), calls=%async_computation.3 | async-start | bytes 524288 | tf_op jit(solution)/shard_map/all_to_all | solution.py:637
  174.0 0.7 copy-start.1

commit v4 on v3

--- a/solution.py
+++ b/solution.py
@@ -191,7 +191,7 @@
         out_ref[here, :] = dot(jnp.concatenate(onehot, axis=1), mapped_ref[...]).astype(BF16)
         return carry
 
-    lax.fori_loop(0, many // tall, one, 0)
+    lax.fori_loop(0, many // tall, one, 0, unroll=True)
 
 
 def rank_kernel(me_ref, recv_ref, far_ref, ranks_ref, over_ref, out_ref, mapped_ref, done, *, users, cap, mask):
@@ -229,14 +229,19 @@
     send_set(me, mask, ranks_ref, mapped_ref, out_ref)
 
 
-def index_kernel(me_ref, recv_ref, ranks_ref, over_ref, index_ref, *outs, masks, cap, rows_dev):
+def index_kernel(me_ref, recv_ref, over_ref, index_ref, *, cap, rows_dev):
+    groups, room, users = index_ref.shape
+    for g in range(groups):
+        got = recv_ref[g * users : (g + 1) * users, 0, :]
+        index_ref[g] = index_of(me_ref[0], got, recv_ref.shape[0], cap, room, rows_dev)
+
+
+def places_kernel(me_ref, index_ref, ranks_ref, over_ref, after_ref, order_ref, *outs, masks, rows_dev):
     me = me_ref[0]
-    groups, room, users = index_ref.shape
+    _, room, users = index_ref.shape
     wide = outs[0].shape[1]
     high = rows_dev // 128
-    for g in range(groups):
-        got = recv_ref[g * users : (g + 1) * users, 0, :]
-        index_ref[g] = index_of(me, got, recv_ref.shape[0], cap, room, rows_dev)
+    order_ref[...] = jnp.zeros(order_ref.shape, F32)
     same = iota((room, wide), 0) == iota((room, wide), 1)
     for mask, out_ref in zip(masks, outs):
         plane = div_mod(me, PLANE)[0] ^ mask
@@ -324,10 +329,9 @@
     user_ref[...] = found[owners:].astype(I32)
 
 
-def route(logits_of, rows_refs, user_ref, summed_ref, logits_ref):
-    owners = len(rows_refs)
+def route(logits_of, rows_refs, user_ref, summed_ref, logits_ref, blocks=None, more=False):
     lanes = summed_ref.shape[0]
-    for s in range(owners):
+    for s in blocks or range(len(rows_refs)):
         logits = logits_of(s)
         if logits_ref is not None:
             logits_ref[s] = logits
@@ -338,7 +342,7 @@
         weights = raised / jnp.sum(raised, axis=0, keepdims=True)
         spread = jnp.concatenate([jnp.where(user == u + 1, weights, 0.0) for u in range(lanes // caps)], axis=0)
         part = dot(spread.astype(BF16), rows_refs[s][...])
-        if s == 0:
+        if s == 0 and not more:
             summed_ref[...] = part
         else:
             summed_ref[...] += part
@@ -369,18 +373,32 @@
         sent_ref[lanes:, room:] = jnp.zeros((sent_ref.shape[0] - lanes, sent_ref.shape[1] - room), F32)
 
 
+def flags_of(rows_refs):
+    room = rows_refs[0].shape[0]
+    return sum(ref[room - 16 :, :128].astype(F32) for ref in rows_refs)[15:]
+
+
+def early_kernel(*refs, blocks, first_flag):
+    rows_refs, (seed_ref, user_ref, table_ref, logits_ref, summed_ref, flag_ref) = refs[:blocks], refs[blocks:]
+    _, seeds = table_ref.shape
+    owners, room = seed_ref.shape
+    for s in range(owners):
+        onehot = jnp.where(iota((seeds, room), 0) == seed_ref[s : s + 1, :], 1.0, 0.0)
+        logits_ref[s] = jnp.dot(table_ref[...], onehot, precision=lax.Precision.HIGHEST, preferred_element_type=F32)
+    flag = jnp.zeros((1, 128), F32)
+    if first_flag < blocks:
+        flag = flags_of(rows_refs[first_flag:])
+    flag_ref[...] = jnp.broadcast_to(flag, flag_ref.shape)
+    route(lambda s: logits_ref[s], rows_refs, user_ref, summed_ref, None)
+
+
 def first_kernel(*refs, owners):
-    rows_refs, (seed_ref, user_ref, table_ref, logits_ref, sent_ref, summed_ref, flag_ref) = refs[:owners], refs[owners:]
-    caps, seeds = table_ref.shape
-    room = rows_refs[0].shape[0]
-
-    def initial(s):
-        onehot = jnp.where(iota((seeds, room), 0) == seed_ref[s : s + 1, :], 1.0, 0.0)
-        return jnp.dot(table_ref[...], onehot, precision=lax.Precision.HIGHEST, preferred_element_type=F32)
-
-    flags = sum(ref[room - 16 :, :128].astype(F32) for ref in rows_refs[owners // 2 :])[15:]
-    flag_ref[...] = jnp.broadcast_to(flags, flag_ref.shape)
-    route(initial, rows_refs, user_ref, summed_ref, logits_ref)
+    rows_refs, (user_ref, logits_ref, part_ref, early_ref, sent_ref, summed_ref, flag_ref) = refs[:owners], refs[owners:]
+    caps = logits_ref.shape[1]
+    blocks = range(owners - PLANE, owners)
+    flag_ref[...] = early_ref[...] + jnp.broadcast_to(flags_of(rows_refs[owners - PLANE :]), flag_ref.shape)
+    summed_ref[...] = part_ref[...]
+    route(lambda s: logits_ref[s], rows_refs, user_ref, summed_ref, None, blocks, True)
     products(rows_refs, user_ref, summed_ref, sent_ref, caps)
 
 
@@ -412,7 +430,7 @@
 def squash_kernel(summed_ref, flag_ref, *refs):
     scale = squash_scale(sum(part[:, :1] for part in refs[:-1]))
     scale = jnp.where(flag_ref[0:1, 0:1] > 0.0, jnp.nan, scale)
-    refs[-1][...] = summed_ref[...] * scale
+    refs[-1][...] = (summed_ref[...] * scale).astype(BF16)
 
 
 def call(kernel, out_shape, n_in, smem=(), far=(), far_out=False, flops=0, mib=12, **kw):
@@ -573,14 +591,13 @@
         sets.update({mask: send(x, mask * PLANE) for mask, x in zip(chosen, ready)})
         return order
 
-    index, *places = call(
-        functools.partial(index_kernel, masks=masks, cap=cap, rows_dev=rows_dev),
-        [jax.ShapeDtypeStruct((groups, room, users), F32)] + [jax.ShapeDtypeStruct((8, wide), F32)] * len(masks),
-        4,
+    index = call(
+        functools.partial(index_kernel, cap=cap, rows_dev=rows_dev),
+        jax.ShapeDtypeStruct((groups, room, users), F32),
+        3,
         smem=(0,),
         flops=set_flops,
-    )(here, recv, ranks, over)
-    places = [send(x, mask * PLANE) for mask, x in zip(masks, places)]
+    )(here, recv, over)
     rows = [None] * owners
 
     def near(first, stop, order):
@@ -597,6 +614,14 @@
         return order
 
     order = near(PLANE, owners // 2, index)
+    order, *places = call(
+        functools.partial(places_kernel, masks=masks, rows_dev=rows_dev),
+        [mark] + [jax.ShapeDtypeStruct((8, wide), F32)] * len(masks),
+        5,
+        smem=(0,),
+        flops=set_flops,
+    )(here, index, ranks, over, order)
+    places = [send(x, mask * PLANE) for mask, x in zip(masks, places)]
     order = near(0, PLANE, order)
     where = jax.ShapeDtypeStruct((owners, room), I32)
     seed, user, order = call(
@@ -622,17 +647,21 @@
     summed_shape = jax.ShapeDtypeStruct((lanes, half), F32)
     square_shape = jax.ShapeDtypeStruct((lanes, 128), F32)
     step_shapes = (logits_shape, sent_shape, summed_shape)
+    ready = owners - PLANE
+    kernel = functools.partial(early_kernel, blocks=ready, first_flag=owners // 2)
+    logits, part, flag = call(kernel, (logits_shape, summed_shape, mark), ready + 3)(*rows[:ready], seed, user, seed_table.T)
     kernel = functools.partial(first_kernel, owners=owners)
-    logits, sent, _, flag = call(kernel, step_shapes + (mark,), owners + 3)(*rows, seed, user, seed_table.T)
+    sent, _, flag = call(kernel, (sent_shape, summed_shape, mark), owners + 4)(*rows, user, logits, part, flag)
     later = functools.partial(later_kernel, cols=cols, owners=owners, lanes=lanes)
     for _ in range(ITERS - 2):
         kernel = functools.partial(later, last=False)
         logits, sent, _ = call(kernel, step_shapes, cols + owners + 2)(*all_cols(sent), *rows, user, logits)
     kernel = functools.partial(later, last=True)
     summed, square = call(kernel, (summed_shape, square_shape), cols + owners + 2)(*all_cols(sent), *rows, user, logits)
-    capsules = call(squash_kernel, summed_shape, cols + 2)(summed, flag, *all_cols(square)).reshape(users, caps, half)
+    sent_back = jax.ShapeDtypeStruct((lanes, half), BF16)
+    capsules = call(squash_kernel, sent_back, cols + 2)(summed, flag, *all_cols(square)).reshape(users, caps, half)
     if owners > users:
-        spread = jnp.zeros((owners, caps, half), F32)
+        spread = jnp.zeros((owners, caps, half), BF16)
         capsules = lax.dynamic_update_slice_in_dim(spread, capsules, group, 0)
     back = lax.all_to_all(capsules, "users", split_axis=0, concat_axis=0, tiled=True)
     if owners > users:
@@ -641,7 +670,7 @@
     if owners > users:
         over = lax.pmax(over, "users")
     fits = fits & (over == 0)
-    dealt = back[dest[:, 0]]
+    dealt = back[dest[:, 0]].astype(F32)
 
     def kept(dealt, *_):
         return dealt

time: 175 us -> 171 us (0.977)
  waiting for transfers between devices: 95.2 us -> 91.1 us
    all_to_all x1, waiting for transfers between devices: 8.86 us -> 6.45 us  [on_device(): lax.all_to_all(capsules, 'users', split_axis=0, concat_axis=0, tiled=True)]
    pallas_call x3 -> x5, Pallas kernels: 8.22 us -> 7.98 us  [the longest x1 2.96 us: on_device(): call(functools.partial(places_kernel, masks=masks, rows_dev=rows_dev), [m...]
  transfers between devices with their start and end apart: 23 -> 23, of which waited for: 14 -> 13; matrix products, arithmetic and copies ran while one was open for 0% -> 0% of each run, Pallas kernels for 9% -> 10%
where the time goes in v4:
time: 171 us
  waiting for transfers between devices  91.1 us (53%)
  starting transfers between devices  38.7 us (23%)
  Pallas kernels  37 us (22%)
    ppermute x17, waiting for transfers between devices, send(): return lax.ppermute(x, 'users', [(i, i ^ mask) for i in range(owners)])  78.5 us
    ppermute x17, starting transfers between devices, send(): return lax.ppermute(x, 'users', [(i, i ^ mask) for i in range(owners)])  24.1 us
    all_to_all x1, starting transfers between devices, on_device(): lax.all_to_all(blocks, 'users', split_axis=0, concat_axis=0, tiled=True)  7.85 us
    all_to_all x1, waiting for transfers between devices, on_device(): lax.all_to_all(capsules, 'users', split_axis=0, concat_axis=0, tiled=True)  6.45 us
    pallas_call x2, Pallas kernels, near(): call(functools.partial(near_kernel, first=first), [mark] + [block] * (sto...  6.05 us
    all_to_all x1, starting transfers between devices, on_device(): lax.all_to_all(capsules, 'users', split_axis=0, concat_axis=0, tiled=True)  5.74 us
    pallas_call x1, Pallas kernels, map_table(): call(functools.partial(map_kernel, cols=len(parts)), pltpu.HBM((rows_dev,...  5.07 us
    pallas_call x6, Pallas kernels, on_device(): call(functools.partial(relay_kernel, first=first), [mark] + [block] * (st...  4.22 us
  transfers between devices with their start and end apart: 23, of which 13 were waited for; matrix products, arithmetic and copies ran while one was open for 0% of the time, Pallas kernels for 10%

profile of v4, /device:TPU:0, one launch (start us, length us, event | category | flops | bytes accessed | tf_op | source)
XLA Modules:
  0.0 171.1 jit_solution(3609601292472586401)
XLA Ops:
  0.5 3.4 %shard_map.66 = (s32[16,1,1024]{2,1,0:T(1,128)}, s32[16,1]{1,0:T(8,128)S(1)}) custom-call(s32[1]{0:T(128)} %bitcast.11.local_ref, s32[16,256]{1,0:T(8,128)} %ids_ref.1, s32[16,256]{1,0:T(8,128)} %seeds_ref.1, s32[1,16]{1,0:T(1,128)} %bitcast.66), custom_call_target="tpu_custom_call" | custom-call | bytes 65600 | tf_op jit(solution)/shard_map/pallas_call | solution.py:546
  3.9 7.9 %all-to-all-start.2 = ((s32[16,1,1024]{2,1,0:T(1,128)}), s32[16,1,1024]{2,1,0:T(1,128)S(1)}, u32[]{:S(2)}, u32[]{:S(2)}) async-start(s32[16,1,1024]{2,1,0:T(1,128)} %get-tuple-element.73), calls=%async_computation.2 | async-start | bytes 131072 | tf_op jit(solution)/shard_map/all_to_all | solution.py:552
  11.7 5.1 %shard_map.67.far_ref = bf16[2048,512]{1,0:T(8,128)(2,1)} custom-call(s32[1]{0:T(128)} %bitcast.14.refs_0_, bf16[1024,512]{1,0:T(8,128)(2,1)} %refs_1_.1, bf16[2048,512]{1,0:T(8,128)(2,1)} %refs_2_.1, bf16[2048,512]{1,0:T(8,128)(2,1)S(1)} %collective-permute-done.6.refs_3_), custom_call_target="tpu_custom_call" | custom-call | flops 2147483648 | bytes 2097152 | tf_op jit(solution)/shard_map/pallas_call | solution.py:503
  16.8 2.4 %all-to-all-done.2.recv_ref = s32[16,1,1024]{2,1,0:T(1,128)S(1)} async-done(((s32[16,1,1024]{2,1,0:T(1,128)}), s32[16,1,1024]{2,1,0:T(1,128)S(1)}, u32[]{:S(2)}, u32[]{:S(2)}) %all-to-all-start.2) | async-done | bytes 65568 | tf_op jit(solution)/shard_map/all_to_all | solution.py:552
  19.3 4.1 %shard_map.68 = (s32[64,128]{1,0:T(8,128)S(1)}, f32[8,128]{1,0:T(8,128)S(1)}, bf16[704,512]{1,0:T(8,128)(2,1)S(1)}, bf16[2048,512]{1,0:T(8,128)(2,1)S(1)}) custom-call(s32[1]{0:T(128)} %bitcast.13.me_ref, s32[16,1,1024]{2,1,0:T(1,128)S(1)} %all-to-all-done.2.recv_ref, bf16[2048,512]{1,0:T(8,128)(2,1)} %shard_map.67.far_ref), custom_call_target="tpu_custom_call" | custom-call | flops 1476395008 | bytes 2854912 | tf_op jit(solution)/shard_map/pallas_call | solution.py:572
  23.3 1.6 shard_map.69.index_ref.after_ref
  25.0 3.0 %shard_map.70 = (f32[8,128]{1,0:T(8,128)S(1)}, bf16[240,512]{1,0:T(8,128)(2,1)S(1)}, bf16[240,512]{1,0:T(8,128)(2,1)S(1)}, bf16[240,512]{1,0:T(8,128)(2,1)S(1)}, bf16[240,512]{1,0:T(8,128)(2,1)S(1)}) custom-call(s32[1]{0:T(128)} %bitcast.13.me_ref, f32[1,240,16]{2,1,0:T(8,128)S(1)} %shard_map.69.index_ref.after_ref, ...), custom_call_target="tpu_custom_call" | custom-call | flops 2013265920 | bytes 987136 | tf_op jit(solution)/shard_map/pallas_call | solution.py:604
  28.0 3.0 %shard_map.71 = (f32[8,128]{1,0:T(8,128)S(1)}, f32[8,256]{1,0:T(8,128)S(1)}, f32[8,256]{1,0:T(8,128)S(1)}) custom-call(s32[1]{0:T(128)} %bitcast.13.me_ref, f32[1,240,16]{2,1,0:T(8,128)S(1)} %shard_map.69.index_ref.after_ref, s32[64,128]{1,0:T(8,128)S(1)} %get-tuple-element.76.ranks_ref, f32[8,128]{1,0:T(8,128)S(1)} %get-tuple-element.74.over_ref, ...), custom_call_target="tpu_custom_call" | custom-call | flops 1476395008 | bytes 20480 | tf_op jit(solution)/shard_map/pallas_call | solution.py:617
  31.0 3.0 %shard_map.72 = (f32[8,128]{1,0:T(8,128)S(1)}, bf16[240,512]{1,0:T(8,128)(2,1)S(1)}, bf16[240,512]{1,0:T(8,128)(2,1)S(1)}, bf16[240,512]{1,0:T(8,128)(2,1)S(1)}, bf16[240,512]{1,0:T(8,128)(2,1)S(1)}) custom-call(s32[1]{0:T(128)} %bitcast.13.me_ref, f32[1,240,16]{2,1,0:T(8,128)S(1)} %shard_map.69.index_ref.after_ref, ...), custom_call_target="tpu_custom_call" | custom-call | flops 2013265920 | bytes 987136 | tf_op jit(solution)/shard_map/pallas_call | solution.py:604
  34.8 1.3 shard_map.73
  36.2 1.7 shard_map.74
  37.8 2.3 %collective-permute-start.19 = (bf16[704,512]{1,0:T(8,128)(2,1)S(1)}, bf16[704,512]{1,0:T(8,128)(2,1)S(1)}, u32[]{:S(2)}, u32[]{:S(2)}) collective-permute-start(bf16[704,512]{1,0:T(8,128)(2,1)S(1)} %get-tuple-element.98), channel_id=1, source_target_pairs={{0,24},{2,26},{4,28},{6,30},{8,16},{10,18},{12,20},{14,22},{16,8},... | collective-permute-start | bytes 2162696 | tf_op jit(solution)/shard_map/ppermute | solution.py:569
  41.9 1.5 collective-permute-start.8
  43.4 55.4 %collective-permute-done.15.places_ref = f32[8,256]{1,0:T(8,128)S(1)} collective-permute-done((f32[8,256]{1,0:T(8,128)S(1)}, f32[8,256]{1,0:T(8,128)S(1)}, u32[]{:S(2)}, u32[]{:S(2)}) %collective-permute-start.15) | collective-permute-done | bytes 8224 | tf_op jit(solution)/shard_map/ppermute | solution.py:569
  98.8 1.2 collective-permute-start.9
  100.1 3.3 %collective-permute-start.20 = (f32[8,256]{1,0:T(8,128)S(1)}, f32[8,256]{1,0:T(8,128)S(1)}, u32[]{:S(2)}, u32[]{:S(2)}) collective-permute-start(f32[8,256]{1,0:T(8,128)S(1)} %get-tuple-element.99), channel_id=1, source_target_pairs={{0,24},{2,26},{4,28},{6,30},{8,16},{10,18},{12,20},{14,22},{16,8},... | collective-permute-start | bytes 24584 | tf_op jit(solution)/shard_map/ppermute | solution.py:569
  103.8 1.7 %collective-permute-done.20.places_ref = f32[8,256]{1,0:T(8,128)S(1)} collective-permute-done((f32[8,256]{1,0:T(8,128)S(1)}, f32[8,256]{1,0:T(8,128)S(1)}, u32[]{:S(2)}, u32[]{:S(2)}) %collective-permute-start.20) | collective-permute-done | bytes 8224 | tf_op jit(solution)/shard_map/ppermute | solution.py:569
  105.5 2.6 %collective-permute-start.11 = (bf16[240,512]{1,0:T(8,128)(2,1)S(1)}, bf16[240,512]{1,0:T(8,128)(2,1)S(1)}, u32[]{:S(2)}, u32[]{:S(2)}) collective-permute-start(bf16[240,512]{1,0:T(8,128)(2,1)S(1)} %get-tuple-element.84), channel_id=1, source_target_pairs={{0,10},{2,8},{4,14},{6,12},{8,2},{10,0},{12,6},{14,4},{16,26},{18,... | collective-permute-start | bytes 737288 | tf_op jit(solution)/shard_map/ppermute | solution.py:569
  109.7 2.7 %collective-permute-start.13 = (bf16[240,512]{1,0:T(8,128)(2,1)S(1)}, bf16[240,512]{1,0:T(8,128)(2,1)S(1)}, u32[]{:S(2)}, u32[]{:S(2)}) collective-permute-start(bf16[240,512]{1,0:T(8,128)(2,1)S(1)} %get-tuple-element.86), channel_id=1, source_target_pairs={{0,14},{2,12},{4,10},{6,8},{8,6},{10,4},{12,2},{14,0},{16,30},{18,... | collective-permute-start | bytes 737288 | tf_op jit(solution)/shard_map/ppermute | solution.py:569
  114.3 1.7 collective-permute-start.18
  116.0 4.2 %collective-permute-done.11.refs_5_.refs_7_ = bf16[240,512]{1,0:T(8,128)(2,1)S(1)} collective-permute-done((bf16[240,512]{1,0:T(8,128)(2,1)S(1)}, bf16[240,512]{1,0:T(8,128)(2,1)S(1)}, u32[]{:S(2)}, u32[]{:S(2)}) %collective-permute-start.11) | collective-permute-done | bytes 245792 | tf_op jit(solution)/shard_map/ppermute | solution.py:569
  122.3 3.8 %collective-permute-done.12.refs_6_.refs_8_ = bf16[240,512]{1,0:T(8,128)(2,1)S(1)} collective-permute-done((bf16[240,512]{1,0:T(8,128)(2,1)S(1)}, bf16[240,512]{1,0:T(8,128)(2,1)S(1)}, u32[]{:S(2)}, u32[]{:S(2)}) %collective-permute-start.12) | collective-permute-done | bytes 245792 | tf_op jit(solution)/shard_map/ppermute | solution.py:569
  127.0 2.1 %collective-permute-done.13.refs_7_.refs_9_ = bf16[240,512]{1,0:T(8,128)(2,1)S(1)} collective-permute-done((bf16[240,512]{1,0:T(8,128)(2,1)S(1)}, bf16[240,512]{1,0:T(8,128)(2,1)S(1)}, u32[]{:S(2)}, u32[]{:S(2)}) %collective-permute-start.13) | collective-permute-done | bytes 245792 | tf_op jit(solution)/shard_map/ppermute | solution.py:569
  129.1 1.3 collective-permute-start.23
  130.4 8.5 %collective-permute-done.17.refs_10_.refs_12_ = bf16[240,512]{1,0:T(8,128)(2,1)S(1)} collective-permute-done((bf16[240,512]{1,0:T(8,128)(2,1)S(1)}, bf16[240,512]{1,0:T(8,128)(2,1)S(1)}, u32[]{:S(2)}, u32[]{:S(2)}) %collective-permute-start.17) | collective-permute-done | bytes 245792 | tf_op jit(solution)/shard_map/ppermute | solution.py:569
  138.9 1.5 collective-permute-start.21
  143.5 1.6 collective-permute-done.21.refs_13_.refs_15_
  145.1 1.5 shard_map.82
  146.7 1.3 collective-permute-done.24.refs_1_
  148.0 2.3 %shard_map.83 = (f32[16,8,240]{2,1,0:T(8,128)S(1)}, f32[128,256]{1,0:T(8,128)S(1)}, f32[128,512]{1,0:T(8,128)}) custom-call(f32[128,256]{1,0:T(8,128)S(1)} %get-tuple-element.112.refs_0_, f32[128,256]{1,0:T(8,128)S(1)} %collective-permute-done.24.refs_1_, bf16[240,512]{1,0:T(8,128)(2,1)S(1)} %get-tuple-element.79.refs_0_.refs_2_, ...), custom_call_target="tpu_custom_call" | custom-call | bytes 516096 | tf_op jit(solution)/shard_map/pallas_call | solution.py:658
  154.9 5.7 %all-to-all-start.3 = ((bf16[16,8,512]{2,1,0:T(8,128)(2,1)}), bf16[16,8,512]{2,1,0:T(8,128)(2,1)S(1)}, u32[]{:S(2)}, u32[]{:S(2)}) async-start(bf16[16,8,512]{2,1,0:T(8,128)(2,1)} %bitcast.16), calls=%async_computation.3 | async-start | bytes 262144 | tf_op jit(solution)/shard_map/all_to_all | solution.py:666
  162.0 6.4 %all-to-all-done.3 = bf16[16,8,512]{2,1,0:T(8,128)(2,1)S(1)} async-done(((bf16[16,8,512]{2,1,0:T(8,128)(2,1)}), bf16[16,8,512]{2,1,0:T(8,128)(2,1)S(1)}, u32[]{:S(2)}, u32[]{:S(2)}) %all-to-all-start.3) | async-done | bytes 131104 | tf_op jit(solution)/shard_map/all_to_all | solution.py:666
  (52 shorter events, 20.6 us)
Async XLA Ops:
  0.0 11.7 %collective-permute-start.6 = (bf16[2048,512]{1,0:T(8,128)(2,1)}, bf16[2048,512]{1,0:T(8,128)(2,1)S(1)}, u32[]{:S(2)}, u32[]{:S(2)}) collective-permute-start(bf16[2048,512]{1,0:T(8,128)(2,1)} %refs_2_.1), channel_id=1, source_target_pairs={{1,0},{0,1},{3,2},{2,3},{5,4},{4,5},{7,6},{6,7},{9,8},{8,9},{11,10... | collective-permute-start | bytes 6291464 | tf_op jit(solution)/shard_map/ppermute | solution.py:452
  3.9 15.4 %all-to-all-start.2 = ((s32[16,1,1024]{2,1,0:T(1,128)}), s32[16,1,1024]{2,1,0:T(1,128)S(1)}, u32[]{:S(2)}, u32[]{:S(2)}) async-start(s32[16,1,1024]{2,1,0:T(1,128)} %get-tuple-element.73), calls=%async_computation.2 | async-start | bytes 131072 | tf_op jit(solution)/shard_map/all_to_all | solution.py:552
  34.0 66.0 %collective-permute-start.14 = (bf16[704,512]{1,0:T(8,128)(2,1)S(1)}, bf16[704,512]{1,0:T(8,128)(2,1)S(1)}, u32[]{:S(2)}, u32[]{:S(2)}) collective-permute-start(bf16[704,512]{1,0:T(8,128)(2,1)S(1)} %get-tuple-element.87), channel_id=1, source_target_pairs={{0,16},{2,18},{4,20},{6,22},{8,24},{10,26},{12,28},{14,30},{16,0},... | collective-permute-start | bytes 2162696 | tf_op jit(solution)/shard_map/ppermute | solution.py:569
  36.1 105.0 %copy-start.4 = (f32[64,8]{0,1:T(8,128)S(1)}, f32[64,8]{0,1:T(8,128)}, u32[]{:S(2)}) copy-start(f32[64,8]{0,1:T(8,128)} %param.13) | copy-start | bytes 6148
  37.8 74.6 %collective-permute-start.19 = (bf16[704,512]{1,0:T(8,128)(2,1)S(1)}, bf16[704,512]{1,0:T(8,128)(2,1)S(1)}, u32[]{:S(2)}, u32[]{:S(2)}) collective-permute-start(bf16[704,512]{1,0:T(8,128)(2,1)S(1)} %get-tuple-element.98), channel_id=1, source_target_pairs={{0,24},{2,26},{4,28},{6,30},{8,16},{10,18},{12,20},{14,22},{16,8},... | collective-permute-start | bytes 2162696 | tf_op jit(solution)/shard_map/ppermute | solution.py:569
  40.2 65.4 %collective-permute-start.7 = (bf16[240,512]{1,0:T(8,128)(2,1)S(1)}, bf16[240,512]{1,0:T(8,128)(2,1)S(1)}, u32[]{:S(2)}, u32[]{:S(2)}) collective-permute-start(bf16[240,512]{1,0:T(8,128)(2,1)S(1)} %get-tuple-element.80), channel_id=1, source_target_pairs={{0,2},{2,0},{4,6},{6,4},{8,10},{10,8},{12,14},{14,12},{16,18},{18,... | collective-permute-start | bytes 737288 | tf_op jit(solution)/shard_map/ppermute | solution.py:569
  40.7 58.1 %collective-permute-start.15 = (f32[8,256]{1,0:T(8,128)S(1)}, f32[8,256]{1,0:T(8,128)S(1)}, u32[]{:S(2)}, u32[]{:S(2)}) collective-permute-start(f32[8,256]{1,0:T(8,128)S(1)} %get-tuple-element.88), channel_id=1, source_target_pairs={{0,16},{2,18},{4,20},{6,22},{8,24},{10,26},{12,28},{14,30},{16,0},... | collective-permute-start | bytes 24584 | tf_op jit(solution)/shard_map/ppermute | solution.py:569
  41.9 67.1 %collective-permute-start.8 = (bf16[240,512]{1,0:T(8,128)(2,1)S(1)}, bf16[240,512]{1,0:T(8,128)(2,1)S(1)}, u32[]{:S(2)}, u32[]{:S(2)}) collective-permute-start(bf16[240,512]{1,0:T(8,128)(2,1)S(1)} %get-tuple-element.81), channel_id=1, source_target_pairs={{0,4},{2,6},{4,0},{6,2},{8,12},{10,14},{12,8},{14,10},{16,20},{18,... | collective-permute-start | bytes 737288 | tf_op jit(solution)/shard_map/ppermute | solution.py:569
  98.8 10.9 %collective-permute-start.9 = (bf16[240,512]{1,0:T(8,128)(2,1)S(1)}, bf16[240,512]{1,0:T(8,128)(2,1)S(1)}, u32[]{:S(2)}, u32[]{:S(2)}) collective-permute-start(bf16[240,512]{1,0:T(8,128)(2,1)S(1)} %get-tuple-element.82), channel_id=1, source_target_pairs={{0,6},{2,4},{4,2},{6,0},{8,14},{10,12},{12,10},{14,8},{16,22},{18,... | collective-permute-start | bytes 737288 | tf_op jit(solution)/shard_map/ppermute | solution.py:569
  100.1 5.4 %collective-permute-start.20 = (f32[8,256]{1,0:T(8,128)S(1)}, f32[8,256]{1,0:T(8,128)S(1)}, u32[]{:S(2)}, u32[]{:S(2)}) collective-permute-start(f32[8,256]{1,0:T(8,128)S(1)} %get-tuple-element.99), channel_id=1, source_target_pairs={{0,24},{2,26},{4,28},{6,30},{8,16},{10,18},{12,20},{14,22},{16,8},... | collective-permute-start | bytes 24584 | tf_op jit(solution)/shard_map/ppermute | solution.py:569
  105.5 8.8 %collective-permute-start.10 = (bf16[240,512]{1,0:T(8,128)(2,1)S(1)}, bf16[240,512]{1,0:T(8,128)(2,1)S(1)}, u32[]{:S(2)}, u32[]{:S(2)}) collective-permute-start(bf16[240,512]{1,0:T(8,128)(2,1)S(1)} %get-tuple-element.83), channel_id=1, source_target_pairs={{0,8},{2,10},{4,12},{6,14},{8,0},{10,2},{12,4},{14,6},{16,24},{18,... | collective-permute-start | bytes 737288 | tf_op jit(solution)/shard_map/ppermute | solution.py:569
  105.5 14.7 %collective-permute-start.11 = (bf16[240,512]{1,0:T(8,128)(2,1)S(1)}, bf16[240,512]{1,0:T(8,128)(2,1)S(1)}, u32[]{:S(2)}, u32[]{:S(2)}) collective-permute-start(bf16[240,512]{1,0:T(8,128)(2,1)S(1)} %get-tuple-element.84), channel_id=1, source_target_pairs={{0,10},{2,8},{4,14},{6,12},{8,2},{10,0},{12,6},{14,4},{16,26},{18,... | collective-permute-start | bytes 737288 | tf_op jit(solution)/shard_map/ppermute | solution.py:569
  109.0 17.0 %collective-permute-start.12 = (bf16[240,512]{1,0:T(8,128)(2,1)S(1)}, bf16[240,512]{1,0:T(8,128)(2,1)S(1)}, u32[]{:S(2)}, u32[]{:S(2)}) collective-permute-start(bf16[240,512]{1,0:T(8,128)(2,1)S(1)} %get-tuple-element.85), channel_id=1, source_target_pairs={{0,12},{2,14},{4,8},{6,10},{8,4},{10,6},{12,0},{14,2},{16,28},{18,... | collective-permute-start | bytes 737288 | tf_op jit(solution)/shard_map/ppermute | solution.py:569
  109.7 19.4 %collective-permute-start.13 = (bf16[240,512]{1,0:T(8,128)(2,1)S(1)}, bf16[240,512]{1,0:T(8,128)(2,1)S(1)}, u32[]{:S(2)}, u32[]{:S(2)}) collective-permute-start(bf16[240,512]{1,0:T(8,128)(2,1)S(1)} %get-tuple-element.86), channel_id=1, source_target_pairs={{0,14},{2,12},{4,10},{6,8},{8,6},{10,4},{12,2},{14,0},{16,30},{18,... | collective-permute-start | bytes 737288 | tf_op jit(solution)/shard_map/ppermute | solution.py:569
  112.4 26.5 %collective-permute-start.17 = (bf16[240,512]{1,0:T(8,128)(2,1)S(1)}, bf16[240,512]{1,0:T(8,128)(2,1)S(1)}, u32[]{:S(2)}, u32[]{:S(2)}) collective-permute-start(bf16[240,512]{1,0:T(8,128)(2,1)S(1)} %get-tuple-element.96), channel_id=1, source_target_pairs={{0,4},{2,6},{4,0},{6,2},{8,12},{10,14},{12,8},{14,10},{16,20},{18,... | collective-permute-start | bytes 737288 | tf_op jit(solution)/shard_map/ppermute | solution.py:569
  114.3 26.8 %collective-permute-start.18 = (bf16[240,512]{1,0:T(8,128)(2,1)S(1)}, bf16[240,512]{1,0:T(8,128)(2,1)S(1)}, u32[]{:S(2)}, u32[]{:S(2)}) collective-permute-start(bf16[240,512]{1,0:T(8,128)(2,1)S(1)} %get-tuple-element.97), channel_id=1, source_target_pairs={{0,6},{2,4},{4,2},{6,0},{8,14},{10,12},{12,10},{14,8},{16,22},{18,... | collective-permute-start | bytes 737288 | tf_op jit(solution)/shard_map/ppermute | solution.py:569
  120.2 20.9 %collective-permute-start.16 = (bf16[240,512]{1,0:T(8,128)(2,1)S(1)}, bf16[240,512]{1,0:T(8,128)(2,1)S(1)}, u32[]{:S(2)}, u32[]{:S(2)}) collective-permute-start(bf16[240,512]{1,0:T(8,128)(2,1)S(1)} %get-tuple-element.95), channel_id=1, source_target_pairs={{0,2},{2,0},{4,6},{6,4},{8,10},{10,8},{12,14},{14,12},{16,18},{18,... | collective-permute-start | bytes 737288 | tf_op jit(solution)/shard_map/ppermute | solution.py:569
  126.1 17.4 %collective-permute-start.22 = (bf16[240,512]{1,0:T(8,128)(2,1)S(1)}, bf16[240,512]{1,0:T(8,128)(2,1)S(1)}, u32[]{:S(2)}, u32[]{:S(2)}) collective-permute-start(bf16[240,512]{1,0:T(8,128)(2,1)S(1)} %get-tuple-element.105), channel_id=1, source_target_pairs={{0,4},{2,6},{4,0},{6,2},{8,12},{10,14},{12,8},{14,10},{16,20},{18,... | collective-permute-start | bytes 737288 | tf_op jit(solution)/shard_map/ppermute | solution.py:569
  129.1 14.4 %collective-permute-start.23 = (bf16[240,512]{1,0:T(8,128)(2,1)S(1)}, bf16[240,512]{1,0:T(8,128)(2,1)S(1)}, u32[]{:S(2)}, u32[]{:S(2)}) collective-permute-start(bf16[240,512]{1,0:T(8,128)(2,1)S(1)} %get-tuple-element.106), channel_id=1, source_target_pairs={{0,6},{2,4},{4,2},{6,0},{8,14},{10,12},{12,10},{14,8},{16,22},{18,... | collective-permute-start | bytes 737288 | tf_op jit(solution)/shard_map/ppermute | solution.py:569
  138.9 6.2 %collective-permute-start.21 = (bf16[240,512]{1,0:T(8,128)(2,1)S(1)}, bf16[240,512]{1,0:T(8,128)(2,1)S(1)}, u32[]{:S(2)}, u32[]{:S(2)}) collective-permute-start(bf16[240,512]{1,0:T(8,128)(2,1)S(1)} %get-tuple-element.104), channel_id=1, source_target_pairs={{0,2},{2,0},{4,6},{6,4},{8,10},{10,8},{12,14},{14,12},{16,18},{18,... | collective-permute-start | bytes 737288 | tf_op jit(solution)/shard_map/ppermute | solution.py:569
  146.6 23.7 %copy-start.2 = (s32[16,256]{1,0:T(8,128)S(1)}, s32[16,256]{1,0:T(8,128)}, u32[]{:S(2)}) copy-start(s32[16,256]{1,0:T(8,128)} %ids_ref.1) | copy-start | bytes 49156
  146.6 23.7 %copy-start.3 = (s32[16,256]{1,0:T(8,128)S(1)}, s32[16,256]{1,0:T(8,128)}, u32[]{:S(2)}) copy-start(s32[16,256]{1,0:T(8,128)} %seeds_ref.1) | copy-start | bytes 49156
  146.6 23.7 %copy-start.5 = (s32[16]{0:T(128)S(1)}, s32[16]{0:T(128)}, u32[]{:S(2)}) copy-start(s32[16]{0:T(128)} %param.9) | copy-start | bytes 196
  146.6 1.4 collective-permute-start.24
  150.3 1.4 collective-permute-start.25
  152.8 1.3 collective-permute-start.26
  154.9 13.5 %all-to-all-start.3 = ((bf16[16,8,512]{2,1,0:T(8,128)(2,1)}), bf16[16,8,512]{2,1,0:T(8,128)(2,1)S(1)}, u32[]{:S(2)}, u32[]{:S(2)}) async-start(bf16[16,8,512]{2,1,0:T(8,128)(2,1)} %bitcast.16), calls=%async_computation.3 | async-start | bytes 262144 | tf_op jit(solution)/shard_map/all_to_all | solution.py:666
  170.4 0.7 copy-start.1
